TPU v7x, 32 devices: a whole 2x2x4 slice. The times are simulated.
32 devices in a mesh: lon: 16 (over z, x, core), lat: 2 (over y).
Axes of the slice: x: 2, y: 2, z: 4, core: 2. Of those that a mesh axis runs over, the one named last changes fastest.
Arguments:
- zonal_state: float32 [4, 32, 3, 8, 2048], P(None, None, None, 'lat', 'lon'), may hold values from -6 to 6
- zonal_courant: float32 [32, 8, 2048], P(None, 'lat', 'lon'), may hold values from -0.5 to 0.5
- zonal_length: int32 [8], P('lat'), may hold values from 512 to 2048, as said below
- zonal_owner: int32 [8, 2048], P('lat', 'lon'), may hold values from 0 to 63, as said below
- merid_state: float32 [4, 32, 3, 64, 256], P(None, None, None, 'lon', 'lat'), may hold values from -6 to 6
- merid_courant: float32 [32, 64, 256], P(None, 'lon', 'lat'), may hold values from -0.5 to 0.5
- mixing: float32 [4, 32, 32], replicated, may hold values from -0.18 to 0.18
Outputs:
- zonal_next: float32 [4, 32, 3, 8, 2048], P(None, None, None, 'lat', 'lon')
- merid_next: float32 [4, 32, 3, 64, 256], P(None, None, None, 'lon', 'lat')
- coupling: float32 [64, 8, 128], P('lon', 'lat')
Inputs may be any that keep to these rules, and one draw needn't show every extreme that they name: `zonal_owner`: non-decreasing along each row; each GCM column holds 16 to 48 consecutive cells of a row, and cell x belongs to a column g with |g - x // 32| <= 1. `zonal_length`: in each latitude sector (aligned blocks of 4 cycles) the first cycle holds 1088 cells and the second 2048.
All inputs are finite; a program needn't handle non-finite values.
Results may differ from a plain program's by a relative error of at most 0.0003.
Values sent between devices are 32-bit elements; how exact they have to be, the bound alone decides.
No kernel may reach another device: no remote copies, remote signals or barrier semaphores. Data moves between devices by JAX's collectives and lax.ppermute only.
A program may use at most 64 MiB of HBM per device.

v0:
```python
import jax
import jax.numpy as jnp
from jax import lax
from jax.sharding import PartitionSpec as P

SUB = 4
CELLS_DEV = 128
GLON_DEV = 4


diffuse_along = 0.3
diffuse_across = 0.1


def padded_2(cells, sides, width, closed):
    for axis, dim in sides:
        count = lax.axis_size(axis)
        ends = count if closed else count - 1
        head = lax.slice_in_dim(cells, 0, width, axis=dim)
        tail = lax.slice_in_dim(cells, cells.shape[dim] - width, cells.shape[dim], axis=dim)
        cells = jnp.concatenate(
            [
                lax.ppermute(tail, axis, [(i, (i + 1) % count) for i in range(ends)]),
                cells,
                lax.ppermute(head, axis, [((i + 1) % count, i) for i in range(ends)]),
            ],
            axis=dim,
        )
    return cells


def from_behind(value, axis, steps):
    count = lax.axis_size(axis)
    pairs = [(source, (source + steps) % count) for source in range(count)]
    return lax.ppermute(value, axis, pairs)


def across_terms(field_now):
    plus_side = jnp.concatenate([field_now[:, :, 1:], field_now[:, :, 2:3]], axis=2)
    minus_side = jnp.concatenate([field_now[:, :, 0:1], field_now[:, :, :2]], axis=2)
    return diffuse_across * (plus_side + minus_side - 2.0 * field_now)


def tendency(field_now, forward_side, backward_side, courant, mixing):
    vertical = jnp.einsum("vkj,vjwrx->vkwrx", mixing, field_now, precision=lax.Precision.HIGHEST)
    advect = -0.5 * courant * (forward_side - backward_side)
    spread = diffuse_along * (forward_side - 2.0 * field_now + backward_side)
    return advect + spread + across_terms(field_now) + vertical


def cycle_ends(own_now, lon_index, own_tail):
    head_part = jnp.where(lon_index == 0, own_now[..., 0], 0.0)
    tail_part = jnp.sum(jnp.where(own_tail, own_now, 0.0), axis=-1)
    return lax.psum((head_part, tail_part), "lon")


def shards(
    zonal_state, zonal_courant, zonal_length, zonal_owner, merid_state, merid_courant, mixing
):
    rows_dev = zonal_state.shape[3]
    cells_dev = zonal_state.shape[4]
    lon_index = lax.axis_index("lon")
    lat_index = lax.axis_index("lat")
    lat_count = lax.axis_size("lat")
    cycle_total = cells_dev * lax.axis_size("lon")
    cells = lon_index * cells_dev + jnp.arange(cells_dev, dtype=jnp.int32)
    own_tail = cells[None, :] == zonal_length[:, None] - 1
    extended = jnp.mod(
        lon_index * cells_dev - SUB + jnp.arange(cells_dev + 2 * SUB, dtype=jnp.int32), cycle_total
    )
    at_tail = extended[None, :] == zonal_length[:, None] - 1
    at_head = extended[None, :] == 0
    active = extended[None, :] < zonal_length[:, None]
    zonal_now, courant_wide = (
        padded_2(zonal_state, (("lon", 4),), SUB, True),
        padded_2(zonal_courant[None, :, None], (("lon", 4),), SUB, True),
    )
    courant_wide = courant_wide[0]
    for substep in range(SUB):
        head_cell, tail_cell = cycle_ends(
            zonal_now[..., SUB : SUB + cells_dev], lon_index, own_tail
        )
        forward_side = jnp.concatenate([zonal_now[..., 1:], zonal_now[..., -1:]], axis=-1)
        backward_side = jnp.concatenate([zonal_now[..., :1], zonal_now[..., :-1]], axis=-1)
        forward_side = jnp.where(at_tail, head_cell[..., None], forward_side)
        backward_side = jnp.where(at_head, tail_cell[..., None], backward_side)
        change = tendency(zonal_now, forward_side, backward_side, courant_wide, mixing)
        zonal_now = jnp.where(active, zonal_now + change, zonal_now)
    zonal_now = zonal_now[..., SUB : SUB + cells_dev]
    merid_now = merid_state
    for substep in range(SUB):
        padded = padded_2(merid_now, (("lat", 4),), 1, False)
        north_edge, south_edge = from_behind(
            (merid_now[:, :, ::-1, :, -1], merid_now[:, :, ::-1, :, 0]),
            "lon",
            lax.axis_size("lon") // 2,
        )
        forward_side = padded[..., 2:]
        backward_side = padded[..., :-2]
        forward_side = forward_side.at[..., -1].set(
            jnp.where(lat_index == lat_count - 1, north_edge, forward_side[..., -1])
        )
        backward_side = backward_side.at[..., 0].set(
            jnp.where(lat_index == 0, south_edge, backward_side[..., 0])
        )
        merid_now = merid_now + tendency(
            merid_now, forward_side, backward_side, merid_courant[:, None], mixing
        )
    scale = GLON_DEV / (3.0 * CELLS_DEV)
    change_sum = jnp.sum(zonal_now - zonal_state, axis=2) * scale
    flat = change_sum.reshape(-1, rows_dev, cells_dev)
    nearby = lon_index * GLON_DEV - 1 + jnp.arange(GLON_DEV + 2, dtype=jnp.int32)
    near_table = (zonal_owner[:, :, None] == nearby[None, None, :]).astype(jnp.float32)
    near_terms = jnp.einsum("rxg,jrx->grj", near_table, flat, precision=lax.Precision.HIGHEST)
    widened = padded_2(near_terms, (("lon", 0),), 1, False)
    coupling = widened[2:-2]
    coupling = coupling.at[0].add(widened[0]).at[-1].add(widened[-1])
    return (zonal_now, merid_now, coupling)


def solution(mesh):
    return jax.shard_map(
        shards,
        mesh=mesh,
        in_specs=(
            P(None, None, None, "lat", "lon"),
            P(None, "lat", "lon"),
            P("lat"),
            P("lat", "lon"),
            P(None, None, None, "lon", "lat"),
            P(None, "lon", "lat"),
            P(),
        ),
        out_specs=(
            P(None, None, None, "lat", "lon"),
            P(None, None, None, "lon", "lat"),
            P("lon", "lat", None),
        ),
        check_vma=False,
    )
```

profile of v0, /device:TPU:0, one launch (start us, length us, event | category | flops | bytes accessed | tf_op | source)
XLA Modules:
  0.0 459.2 jit_solution(1524387161490078369)
XLA Ops:
  4.8 2.6 collective-permute-start.2
  7.4 2.4 collective-permute-start.3
  13.5 5.8 %collective-permute-start.6 = (f32[4,32,3,4,1]{1,3,4,2,0:T(4,128)}, f32[4,32,3,4,1]{1,3,4,2,0:T(4,128)}, u32[]{:S(2)}, u32[]{:S(2)}) collective-permute-start(f32[4,32,3,4,1]{1,3,4,2,0:T(4,128)} %copy.1002), channel_id=1, source_target_pairs={{0,1},{2,3},{4,5},{6,7},{8,9},{10,11},{12,13},{14,15},{16,17},{18,... | collective-permute-start | bytes 18440 | tf_op jit(solution)/shard_map/ppermute | solution.py:23
  28.8 58.5 %all-reduce.3 = (f32[4,32,3,4]{1,3,2,0:T(4,128)}, f32[4,32,3,4]{1,3,2,0:T(4,128)}) all-reduce(f32[4,32,3,4]{1,3,2,0:T(4,128)} %get-tuple-element.279, f32[4,32,3,4]{1,3,2,0:T(4,128)S(1)} %fusion.28), channel_id=1, replica_groups=mesh['lon'=16,'lat'=2] {'lon'}, use_global_device_ids=true, to_apply=%region_2.3 | all-reduce | flops 3072 | bytes 24576 | tf_op jit(solution)/shard_map/psum | solution.py:54
  89.1 2.9 collective-permute-start.7
  102.0 3.2 pad_maximum_fusion.8
  105.2 2.5 scatter.29
  107.7 4.4 scatter.26
  113.0 2.8 fusion.12
  121.5 4.8 %collective-permute-start.10 = (f32[4,32,3,4,1]{1,3,4,2,0:T(4,128)S(1)}, f32[4,32,3,4,1]{1,3,4,2,0:T(4,128)S(1)}, u32[]{:S(2)}, u32[]{:S(2)}) collective-permute-start(f32[4,32,3,4,1]{1,3,4,2,0:T(4,128)S(1)} %copy-done.25), channel_id=1, source_target_pairs={{0,1},{2,3},{4,5},{6,7},{8,9},{10,11},{12,13},{14,15},{16,17},{18,... | collective-permute-start | bytes 18440 | tf_op jit(solution)/shard_map/ppermute | solution.py:23
  126.4 2.5 collective-permute-start.9
  139.6 3.2 pad_maximum_fusion.6
  142.8 5.8 %scatter.30 = f32[4,32,3,4,128]{4,1,3,2,0:T(8,128)} dynamic-update-slice(f32[4,32,3,4,128]{4,1,3,2,0:T(8,128)} %get-tuple-element.263, f32[4,32,3,4,1]{4,1,3,2,0:T(8,128)S(1)} %copy.977, s32[]{:T(128)} %constant.268.clone.1, s32[]{:T(128)} %constant.268.clone.1, s32[]{:T(128)} %constant.268.clone.1, s32[]{:T(128)} %constant.268.clone.1, s32[]{:T(128)} %constant.278.clone.1) | dynamic-update-slice | bytes 12292 | tf_op jit(solution)/shard_map/scatter | solution.py:100
  150.9 2.9 fusion.18
  160.1 4.5 collective-permute-start.14
  164.9 2.4 collective-permute-start.15
  175.4 3.2 pad_maximum_fusion.4
  178.6 5.8 %scatter.34 = f32[4,32,3,4,128]{4,1,3,2,0:T(8,128)} dynamic-update-slice(f32[4,32,3,4,128]{4,1,3,2,0:T(8,128)} %get-tuple-element.255, f32[4,32,3,4,1]{4,1,3,2,0:T(8,128)S(1)} %copy.983, s32[]{:T(128)} %constant.268.clone.1, s32[]{:T(128)} %constant.268.clone.1, s32[]{:T(128)} %constant.268.clone.1, s32[]{:T(128)} %constant.268.clone.1, s32[]{:T(128)} %constant.278.clone.1) | dynamic-update-slice | bytes 12292 | tf_op jit(solution)/shard_map/scatter | solution.py:100
  184.4 2.3 scatter.35
  186.7 2.6 fusion.16
  198.0 6.2 %collective-permute-start.18 = (f32[4,32,3,4,1]{1,3,4,2,0:T(4,128)}, f32[4,32,3,4,1]{1,3,4,2,0:T(4,128)}, u32[]{:S(2)}, u32[]{:S(2)}) collective-permute-start(f32[4,32,3,4,1]{1,3,4,2,0:T(4,128)} %copy.990), channel_id=1, source_target_pairs={{0,1},{2,3},{4,5},{6,7},{8,9},{10,11},{12,13},{14,15},{16,17},{18,... | collective-permute-start | bytes 18440 | tf_op jit(solution)/shard_map/ppermute | solution.py:23
  210.7 2.9 add_select_fusion.2
  221.0 58.3 %all-reduce.2 = (f32[4,32,3,4]{1,3,2,0:T(4,128)}, f32[4,32,3,4]{1,3,2,0:T(4,128)}) all-reduce(f32[4,32,3,4]{1,3,2,0:T(4,128)S(1)} %fusion.26, f32[4,32,3,4]{1,3,2,0:T(4,128)S(1)} %get-tuple-element.232), channel_id=1, replica_groups=mesh['lon'=16,'lat'=2] {'lon'}, use_global_device_ids=true, to_apply=%region_5.6 | all-reduce | flops 3072 | bytes 24576 | tf_op jit(solution)/shard_map/psum | solution.py:54
  279.3 4.6 %add_select_fusion.1 = f32[4,32,3,4,136]{4,1,3,2,0:T(8,128)S(1)} fusion(f32[4,32,3,4,136]{4,1,3,2,0:T(8,128)S(1)} %add_select_fusion.2, f32[4,32,1,4,136]{4,1,3,2,0:T(8,128)} %get-tuple-element.238, f32[4,32,2,4,136]{4,1,3,2,0:T(8,128)} %get-tuple-element.240, f32[4,32,2,4,136]{4,1,3,2,0:T(8,128)} %get-tuple-element.239, ...), kind=kOutput, calls=%fused_computation.1 | convolution fusion | flops 84393984 | bytes 5113032 | tf_op jit(solution)/shard_map/vkj,vjwrx->vkwrx/dot_general | solution.py:45
  291.3 58.6 %all-reduce.1 = (f32[4,32,3,4]{1,3,2,0:T(4,128)}, f32[4,32,3,4]{1,3,2,0:T(4,128)}) all-reduce(f32[4,32,3,4]{1,3,2,0:T(4,128)S(1)} %fusion.24, f32[4,32,3,4]{1,3,2,0:T(4,128)S(1)} %get-tuple-element.223), channel_id=1, replica_groups=mesh['lon'=16,'lat'=2] {'lon'}, use_global_device_ids=true, to_apply=%region_8.9 | all-reduce | flops 3072 | bytes 24576 | tf_op jit(solution)/shard_map/psum | solution.py:54
  349.9 4.6 %add_select_fusion = f32[4,32,3,4,136]{4,1,3,2,0:T(8,128)S(1)} fusion(f32[4,32,3,4,136]{4,1,3,2,0:T(8,128)S(1)} %add_select_fusion.1, f32[4,32,1,4,136]{4,1,3,2,0:T(8,128)} %get-tuple-element.229, f32[4,32,2,4,136]{4,1,3,2,0:T(8,128)} %get-tuple-element.231, f32[4,32,2,4,136]{4,1,3,2,0:T(8,128)} %get-tuple-element.230, ...), kind=kOutput, calls=%fused_computation | convolution fusion | flops 84393984 | bytes 5113032 | tf_op jit(solution)/shard_map/vkj,vjwrx->vkwrx/dot_general | solution.py:45
  357.3 2.4 fusion.23
  362.6 2.6 convolution_bitcast_fusion
  365.3 58.8 %all-reduce = (f32[4,32,3,4]{1,3,2,0:T(4,128)}, f32[4,32,3,4]{1,3,2,0:T(4,128)}) all-reduce(f32[4,32,3,4]{1,3,2,0:T(4,128)} %select_reduce_fusion, f32[4,32,3,4]{1,3,2,0:T(4,128)} %get-tuple-element.214), channel_id=1, replica_groups=mesh['lon'=16,'lat'=2] {'lon'}, use_global_device_ids=true, to_apply=%region_11.12 | all-reduce | flops 3072 | bytes 24576 | tf_op jit(solution)/shard_map/psum | solution.py:54
  441.9 2.9 pad_maximum_fusion.2
  444.9 5.8 %scatter.36 = f32[4,32,3,4,128]{4,1,3,2,0:T(8,128)} dynamic-update-slice(f32[4,32,3,4,128]{4,1,3,2,0:T(8,128)} %get-tuple-element.247, f32[4,32,3,4,1]{4,1,3,2,0:T(8,128)S(1)} %copy.989, s32[]{:T(128)} %constant.268.clone.1, s32[]{:T(128)} %constant.268.clone.1, s32[]{:T(128)} %constant.268.clone.1, s32[]{:T(128)} %constant.268.clone.1, s32[]{:T(128)} %constant.278.clone.1) | dynamic-update-slice | bytes 12292 | tf_op jit(solution)/shard_map/scatter | solution.py:100
  451.8 2.4 fusion.14
  (223 shorter events, 122.4 us)
Async XLA Ops:
  0.6 112.4 %copy-start = (f32[4,32,32]{2,1,0:T(8,128)S(1)}, f32[4,32,32]{2,1,0:T(8,128)}, u32[]{:S(2)}) copy-start(f32[4,32,32]{2,1,0:T(8,128)} %param.33) | copy-start | bytes 49156
  0.7 9.1 %copy-start.3 = (f32[4,32,3,4,128]{4,3,2,1,0:T(4,128)S(1)}, f32[4,32,3,4,128]{4,3,2,1,0:T(4,128)}, u32[]{:S(2)}) copy-start(f32[4,32,3,4,128]{4,3,2,1,0:T(4,128)} %param.31) | copy-start | bytes 2359300
  3.6 201.5 %collective-permute-start = (f32[4,32,3,4,4]{1,4,3,2,0:T(4,128)}, f32[4,32,3,4,4]{1,4,3,2,0:T(4,128)}, u32[]{:S(2)}, u32[]{:S(2)}) collective-permute-start(f32[4,32,3,4,4]{1,4,3,2,0:T(4,128)} %copy.999), channel_id=1, source_target_pairs={{0,2},{2,4},{4,6},{6,8},{8,10},{10,12},{12,14},{14,16},{16,18},{18... | collective-permute-start | bytes 73736 | tf_op jit(solution)/shard_map/ppermute | solution.py:23
  4.8 82.4 %collective-permute-start.2 = (f32[1,32,1,4,4]{4,3,1,2,0:T(4,128)}, f32[1,32,1,4,4]{4,3,1,2,0:T(4,128)}, u32[]{:S(2)}, u32[]{:S(2)}) collective-permute-start(f32[1,32,1,4,4]{4,3,1,2,0:T(4,128)} %get-tuple-element.283), channel_id=1, source_target_pairs={{0,2},{2,4},{4,6},{6,8},{8,10},{10,12},{12,14},{14,16},{16,18},{18... | collective-permute-start | bytes 6152 | tf_op jit(solution)/shard_map/ppermute | solution.py:23
  7.4 79.8 %collective-permute-start.3 = (f32[1,32,1,4,4]{4,3,1,2,0:T(4,128)}, f32[1,32,1,4,4]{4,3,1,2,0:T(4,128)}, u32[]{:S(2)}, u32[]{:S(2)}) collective-permute-start(f32[1,32,1,4,4]{4,3,1,2,0:T(4,128)} %get-tuple-element.284), channel_id=1, source_target_pairs={{2,0},{4,2},{6,4},{8,6},{10,8},{12,10},{14,12},{16,14},{18,16},{20... | collective-permute-start | bytes 6152 | tf_op jit(solution)/shard_map/ppermute | solution.py:25
  11.3 77.9 %collective-permute-start.4 = (f32[4,32,3,4,1]{1,3,4,2,0:T(4,128)}, f32[4,32,3,4,1]{1,3,4,2,0:T(4,128)}, u32[]{:S(2)}, u32[]{:S(2)}) collective-permute-start(f32[4,32,3,4,1]{1,3,4,2,0:T(4,128)} %copy.1001), channel_id=1, source_target_pairs={{1,0},{3,2},{5,4},{7,6},{9,8},{11,10},{13,12},{15,14},{17,16},{19,... | collective-permute-start | bytes 18440 | tf_op jit(solution)/shard_map/ppermute | solution.py:25
  13.5 81.2 %collective-permute-start.6 = (f32[4,32,3,4,1]{1,3,4,2,0:T(4,128)}, f32[4,32,3,4,1]{1,3,4,2,0:T(4,128)}, u32[]{:S(2)}, u32[]{:S(2)}) collective-permute-start(f32[4,32,3,4,1]{1,3,4,2,0:T(4,128)} %copy.1002), channel_id=1, source_target_pairs={{0,1},{2,3},{4,5},{6,7},{8,9},{10,11},{12,13},{14,15},{16,17},{18,... | collective-permute-start | bytes 18440 | tf_op jit(solution)/shard_map/ppermute | solution.py:23
  23.7 4.7 %copy-start.23 = (f32[32,4,128]{2,1,0:T(4,128)S(1)}, f32[32,4,128]{2,1,0:T(4,128)}, u32[]{:S(2)}) copy-start(f32[32,4,128]{2,1,0:T(4,128)} %param.32) | copy-start | bytes 196612
  87.2 119.8 %collective-permute-start.1 = (f32[4,32,3,4,4]{1,4,3,2,0:T(4,128)}, f32[4,32,3,4,4]{1,4,3,2,0:T(4,128)}, u32[]{:S(2)}, u32[]{:S(2)}) collective-permute-start(f32[4,32,3,4,4]{1,4,3,2,0:T(4,128)} %copy.1000), channel_id=1, source_target_pairs={{2,0},{4,2},{6,4},{8,6},{10,8},{12,10},{14,12},{16,14},{18,16},{20... | collective-permute-start | bytes 73736 | tf_op jit(solution)/shard_map/ppermute | solution.py:25
  87.2 5.0 %collective-permute-start.5 = (f32[4,32,3,4]{1,3,2,0:T(4,128)}, f32[4,32,3,4]{1,3,2,0:T(4,128)S(1)}, u32[]{:S(2)}, u32[]{:S(2)}) collective-permute-start(f32[4,32,3,4]{1,3,2,0:T(4,128)} %reverse_bitcast_fusion.1), channel_id=1, source_target_pairs={{0,16},{2,18},{4,20},{6,22},{8,24},{10,26},{12,28},{14,30},{16,0},... | collective-permute-start | bytes 18440 | tf_op jit(solution)/shard_map/ppermute | solution.py:35
  88.4 3.8 copy-start.16
  89.1 5.5 %collective-permute-start.7 = (f32[4,32,3,4]{1,3,2,0:T(4,128)}, f32[4,32,3,4]{1,3,2,0:T(4,128)}, u32[]{:S(2)}, u32[]{:S(2)}) collective-permute-start(f32[4,32,3,4]{1,3,2,0:T(4,128)} %reverse_bitcast_fusion), channel_id=1, source_target_pairs={{0,16},{2,18},{4,20},{6,22},{8,24},{10,26},{12,28},{14,30},{16,0},... | collective-permute-start | bytes 18440 | tf_op jit(solution)/shard_map/ppermute | solution.py:35
  118.0 3.5 copy-start.25
  118.0 8.4 %copy-start.28 = (f32[4,32,3,4]{1,3,2,0:T(4,128)S(1)}, f32[4,32,3,4]{1,3,2,0:T(4,128)}, u32[]{:S(2)}) copy-start(f32[4,32,3,4]{1,3,2,0:T(4,128)} %reverse_reduce_fusion.5) | copy-start | bytes 18436
  120.2 8.9 %collective-permute-start.8 = (f32[4,32,3,4,1]{1,3,4,2,0:T(4,128)S(1)}, f32[4,32,3,4,1]{1,3,4,2,0:T(4,128)S(1)}, u32[]{:S(2)}, u32[]{:S(2)}) collective-permute-start(f32[4,32,3,4,1]{1,3,4,2,0:T(4,128)S(1)} %copy.975), channel_id=1, source_target_pairs={{1,0},{3,2},{5,4},{7,6},{9,8},{11,10},{13,12},{15,14},{17,16},{19,... | collective-permute-start | bytes 18440 | tf_op jit(solution)/shard_map/ppermute | solution.py:25
  121.5 10.3 %collective-permute-start.10 = (f32[4,32,3,4,1]{1,3,4,2,0:T(4,128)S(1)}, f32[4,32,3,4,1]{1,3,4,2,0:T(4,128)S(1)}, u32[]{:S(2)}, u32[]{:S(2)}) collective-permute-start(f32[4,32,3,4,1]{1,3,4,2,0:T(4,128)S(1)} %copy-done.25), channel_id=1, source_target_pairs={{0,1},{2,3},{4,5},{6,7},{8,9},{10,11},{12,13},{14,15},{16,17},{18,... | collective-permute-start | bytes 18440 | tf_op jit(solution)/shard_map/ppermute | solution.py:23
  126.4 5.0 %collective-permute-start.9 = (f32[4,32,3,4]{1,3,2,0:T(4,128)S(1)}, f32[4,32,3,4]{1,3,2,0:T(4,128)S(1)}, u32[]{:S(2)}, u32[]{:S(2)}) collective-permute-start(f32[4,32,3,4]{1,3,2,0:T(4,128)S(1)} %copy-done.28), channel_id=1, source_target_pairs={{0,16},{2,18},{4,20},{6,22},{8,24},{10,26},{12,28},{14,30},{16,0},... | collective-permute-start | bytes 18440 | tf_op jit(solution)/shard_map/ppermute | solution.py:35
  129.1 4.8 %copy-start.19 = (f32[4,32,3,4,1]{1,3,4,2,0:T(4,128)}, f32[4,32,3,4,1]{1,3,4,2,0:T(4,128)S(1)}, u32[]{:S(2)}) copy-start(f32[4,32,3,4,1]{1,3,4,2,0:T(4,128)S(1)} %collective-permute-done.8) | copy-start | bytes 18436
  129.2 4.8 %collective-permute-start.11 = (f32[4,32,3,4]{1,3,2,0:T(4,128)S(1)}, f32[4,32,3,4]{1,3,2,0:T(4,128)S(1)}, u32[]{:S(2)}, u32[]{:S(2)}) collective-permute-start(f32[4,32,3,4]{1,3,2,0:T(4,128)S(1)} %reverse_reduce_fusion.4), channel_id=1, source_target_pairs={{0,16},{2,18},{4,20},{6,22},{8,24},{10,26},{12,28},{14,30},{16,0},... | collective-permute-start | bytes 18440 | tf_op jit(solution)/shard_map/ppermute | solution.py:35
  155.9 4.2 copy-start.26
  158.1 6.8 %collective-permute-start.12 = (f32[4,32,3,4,1]{1,3,4,2,0:T(4,128)S(1)}, f32[4,32,3,4,1]{1,3,4,2,0:T(4,128)S(1)}, u32[]{:S(2)}, u32[]{:S(2)}) collective-permute-start(f32[4,32,3,4,1]{1,3,4,2,0:T(4,128)S(1)} %copy.981), channel_id=1, source_target_pairs={{1,0},{3,2},{5,4},{7,6},{9,8},{11,10},{13,12},{15,14},{17,16},{19,... | collective-permute-start | bytes 18440 | tf_op jit(solution)/shard_map/ppermute | solution.py:25
  159.4 7.9 %collective-permute-start.13 = (f32[4,32,3,4]{1,3,2,0:T(4,128)S(1)}, f32[4,32,3,4]{1,3,2,0:T(4,128)S(1)}, u32[]{:S(2)}, u32[]{:S(2)}) collective-permute-start(f32[4,32,3,4]{1,3,2,0:T(4,128)S(1)} %copy-done.27), channel_id=1, source_target_pairs={{0,16},{2,18},{4,20},{6,22},{8,24},{10,26},{12,28},{14,30},{16,0},... | collective-permute-start | bytes 18440 | tf_op jit(solution)/shard_map/ppermute | solution.py:35
  160.1 7.6 %collective-permute-start.14 = (f32[4,32,3,4,1]{1,3,4,2,0:T(4,128)S(1)}, f32[4,32,3,4,1]{1,3,4,2,0:T(4,128)S(1)}, u32[]{:S(2)}, u32[]{:S(2)}) collective-permute-start(f32[4,32,3,4,1]{1,3,4,2,0:T(4,128)S(1)} %copy-done.26), channel_id=1, source_target_pairs={{0,1},{2,3},{4,5},{6,7},{8,9},{10,11},{12,13},{14,15},{16,17},{18,... | collective-permute-start | bytes 18440 | tf_op jit(solution)/shard_map/ppermute | solution.py:23
  164.9 4.8 %copy-start.20 = (f32[4,32,3,4,1]{1,3,4,2,0:T(4,128)}, f32[4,32,3,4,1]{1,3,4,2,0:T(4,128)S(1)}, u32[]{:S(2)}) copy-start(f32[4,32,3,4,1]{1,3,4,2,0:T(4,128)S(1)} %collective-permute-done.12) | copy-start | bytes 18436
  164.9 4.8 %collective-permute-start.15 = (f32[4,32,3,4]{1,3,2,0:T(4,128)S(1)}, f32[4,32,3,4]{1,3,2,0:T(4,128)S(1)}, u32[]{:S(2)}, u32[]{:S(2)}) collective-permute-start(f32[4,32,3,4]{1,3,2,0:T(4,128)S(1)} %reverse_reduce_fusion.2), channel_id=1, source_target_pairs={{0,16},{2,18},{4,20},{6,22},{8,24},{10,26},{12,28},{14,30},{16,0},... | collective-permute-start | bytes 18440 | tf_op jit(solution)/shard_map/ppermute | solution.py:35
  192.5 241.7 %collective-permute-start.16 = (f32[4,32,3,4,1]{1,3,4,2,0:T(4,128)}, f32[4,32,3,4,1]{1,3,4,2,0:T(4,128)}, u32[]{:S(2)}, u32[]{:S(2)}) collective-permute-start(f32[4,32,3,4,1]{1,3,4,2,0:T(4,128)} %copy.987), channel_id=1, source_target_pairs={{1,0},{3,2},{5,4},{7,6},{9,8},{11,10},{13,12},{15,14},{17,16},{19,... | collective-permute-start | bytes 18440 | tf_op jit(solution)/shard_map/ppermute | solution.py:25
  195.7 240.0 %collective-permute-start.17 = (f32[4,32,3,4]{1,3,2,0:T(4,128)}, f32[4,32,3,4]{1,3,2,0:T(4,128)}, u32[]{:S(2)}, u32[]{:S(2)}) collective-permute-start(f32[4,32,3,4]{1,3,2,0:T(4,128)} %reverse_reduce_fusion.1), channel_id=1, source_target_pairs={{0,16},{2,18},{4,20},{6,22},{8,24},{10,26},{12,28},{14,30},{16,0},... | collective-permute-start | bytes 18440 | tf_op jit(solution)/shard_map/ppermute | solution.py:35
  198.0 238.8 %collective-permute-start.18 = (f32[4,32,3,4,1]{1,3,4,2,0:T(4,128)}, f32[4,32,3,4,1]{1,3,4,2,0:T(4,128)}, u32[]{:S(2)}, u32[]{:S(2)}) collective-permute-start(f32[4,32,3,4,1]{1,3,4,2,0:T(4,128)} %copy.990), channel_id=1, source_target_pairs={{0,1},{2,3},{4,5},{6,7},{8,9},{10,11},{12,13},{14,15},{16,17},{18,... | collective-permute-start | bytes 18440 | tf_op jit(solution)/shard_map/ppermute | solution.py:23
  205.1 231.7 %collective-permute-start.19 = (f32[4,32,3,4]{1,3,2,0:T(4,128)}, f32[4,32,3,4]{1,3,2,0:T(4,128)}, u32[]{:S(2)}, u32[]{:S(2)}) collective-permute-start(f32[4,32,3,4]{1,3,2,0:T(4,128)} %reverse_reduce_fusion), channel_id=1, source_target_pairs={{0,16},{2,18},{4,20},{6,22},{8,24},{10,26},{12,28},{14,30},{16,0},... | collective-permute-start | bytes 18440 | tf_op jit(solution)/shard_map/ppermute | solution.py:35
  432.4 24.6 %collective-permute-start.20 = (f32[1,4,128]{2,0,1:T(1,128)}, f32[1,4,128]{2,0,1:T(1,128)}, u32[]{:S(2)}, u32[]{:S(2)}) collective-permute-start(f32[1,4,128]{2,0,1:T(1,128)} %get-tuple-element.286), channel_id=1, source_target_pairs={{0,2},{2,4},{4,6},{6,8},{8,10},{10,12},{12,14},{14,16},{16,18},{18... | collective-permute-start | bytes 6152 | tf_op jit(solution)/shard_map/ppermute | solution.py:23
  434.2 23.5 %collective-permute-start.21 = (f32[1,4,128]{2,0,1:T(1,128)}, f32[1,4,128]{2,0,1:T(1,128)}, u32[]{:S(2)}, u32[]{:S(2)}) collective-permute-start(f32[1,4,128]{2,0,1:T(1,128)} %get-tuple-element.285), channel_id=1, source_target_pairs={{2,0},{4,2},{6,4},{8,6},{10,8},{12,10},{14,12},{16,14},{18,16},{20... | collective-permute-start | bytes 6152 | tf_op jit(solution)/shard_map/ppermute | solution.py:25
  436.5 5.5 %copy-start.2 = (f32[4,32,3,4,128]{4,1,3,2,0:T(8,128)S(1)}, f32[4,32,3,4,128]{4,1,3,2,0:T(8,128)}, u32[]{:S(2)}) copy-start(f32[4,32,3,4,128]{4,1,3,2,0:T(8,128)} %copy-done.1) | copy-start | bytes 2359300
  (29 other events, 56.8 us)
where the time goes:
time: 468 us; the launch traced here: 459 us
  blocking collectives  234 us (50%)
  local copies, waits for them, and re-layouts  106 us (23%)
  starting transfers between devices  47.3 us (10%)
  other arithmetic  38.5 us (8%)
  matrix products  25.9 us (6%)
  waiting for transfers between devices  6.03 us (1%)
    psum x4, blocking collectives, cycle_ends(): return lax.psum((head_part, tail_part), 'lon')  234 us
    ppermute x7, starting transfers between devices, padded_2(): lax.ppermute(tail, axis, [(i, (i + 1) % count) for i in range(ends)])  26.2 us
    dot_general x8, matrix products, tendency(): jnp.einsum('vkj,vjwrx->vkwrx', mixing, field_now, precision=lax.Precision...  25.6 us
    scatter x4, local copies, waits for them, and re-layouts, shards(): forward_side.at[..., -1]  21.8 us
    concatenate x5, other arithmetic, padded_2(): jnp.concatenate([lax.ppermute(tail, axis, [(i, (i + 1) % count) for i in...  13.2 us
    ppermute x8, starting transfers between devices, from_behind(): return lax.ppermute(value, axis, pairs)  12 us
    unnamed x86, local copies, waits for them, and re-layouts  9.74 us
    slice x8, local copies, waits for them, and re-layouts, across_terms(): field_now[:, :, :2]  9.51 us
  transfers between devices with their start and end apart: 22, of which 4 were waited for; matrix products, arithmetic and copies ran while one was open for 36% of the time, Pallas kernels for 0%

commit v1 on v0

v1 whole, which is shorter than its diff:
```python
import functools

import jax
import jax.numpy as jnp
from jax import lax
from jax.experimental import pallas as pl
from jax.experimental.pallas import tpu as pltpu
from jax.sharding import PartitionSpec as P

SUB = 4
CELLS_DEV = 128
GLON_DEV = 4
DIFFUSE_ALONG = 0.3
DIFFUSE_ACROSS = 0.1
PAD = 4
CHUNK = 10


class Sizes:
    def __init__(self, state_shape):
        self.nv, self.lev, self.wid, self.rows, self.cells = state_shape
        self.lanes = self.nv * self.lev
        self.half = self.cells // 2
        self.span = self.half + 2 * SUB + 2 * PAD
        self.group = 2 * self.rows
        self.wr = self.wid * self.rows
        self.packed = self.wr + self.rows
        self.packet = SUB * self.packed


def turned_courant(sz, ref, r):
    one = ref[pl.ds(r, sz.lev, stride=sz.rows), :]
    return jnp.concatenate([one] * sz.nv, axis=0).T


def put_halves(sz, out_ref, base, r, tile_ref, at):
    n = sz.half + SUB
    first = (base + PAD + SUB) * sz.group + r
    out_ref[pl.ds(first, n, stride=sz.group), :] = tile_ref[at : at + n, :]
    second = (base + PAD) * sz.group + sz.rows + r
    out_ref[pl.ds(second, n, stride=sz.group), :] = tile_ref[
        at + sz.half - SUB : at + sz.cells, :
    ]


def turn_in(sz, lat_two, place, length, z_ref, zc_ref, m_ref, mc_ref, mix_ref,
            zt_ref, zct_ref, mt_ref, mct_ref, w_ref, zfirst, zlast, ht, htp, mlow, mhigh,
            tile, low, high):
    lon = place[0]
    lat = place[1]
    last = place[2]
    edge = 8
    tile[0:edge, :] = jnp.zeros((edge, sz.lanes), jnp.float32)
    tile[edge + sz.cells :, :] = jnp.zeros((edge, sz.lanes), jnp.float32)
    owns_head = jnp.where(lon == 0, 1.0, 0.0).astype(jnp.float32)

    def place_tile(value, slot, r, base, out_ref, zonal):
        tile[edge : edge + sz.cells, :] = value
        put_halves(sz, out_ref, base, r, tile, edge)
        at = pl.ds(slot, SUB, stride=sz.packed)
        begin = tile[edge : edge + SUB, :]
        finish = tile[edge + sz.cells - SUB : edge + sz.cells, :]
        if zonal:
            zfirst[at, :] = begin
            zlast[at, :] = finish
            offset = jnp.clip(length[r] - SUB - lon * sz.cells, -SUB, sz.cells)
            ends = tile[pl.ds(edge + offset, SUB), :]
            ht[at, :] = begin * owns_head
            ht[pl.ds(sz.packet + slot, SUB, stride=sz.packed), :] = ends
        else:
            low[at, :] = begin
            high[at, :] = finish

    for zonal, s_ref, c_ref, st_ref, ct_ref in (
        (False, m_ref, mc_ref, mt_ref, mct_ref), (True, z_ref, zc_ref, zt_ref, zct_ref)
    ):
        for r in range(sz.rows):
            for w in range(sz.wid):
                slot = w * sz.rows + r
                value = s_ref[pl.ds(slot, sz.lanes, stride=sz.wr), :].T
                place_tile(value, slot, r, w * sz.span, st_ref, zonal)
            place_tile(turned_courant(sz, c_ref, r), sz.wr + r, r, 0, ct_ref, zonal)
    htp[0 : 2 * sz.packet, :] = ht[...]
    north = jnp.where(lat == last, 1, 0)
    lows = low[...]
    highs = high[...]
    htp[2 * sz.packet :, :] = jnp.where(north == 1, highs, lows)
    if lat_two:
        mlow[...] = jnp.where(north == 1, lows, highs)
        mhigh[...] = jnp.zeros(mhigh.shape, jnp.float32)
    else:
        mlow[...] = lows
        mhigh[...] = highs
    turned = mix_ref[...].T
    full = jnp.concatenate([turned] * sz.nv, axis=0)
    shape = (sz.lanes, sz.lanes)
    source = lax.broadcasted_iota(jnp.int32, shape, 0)
    target = lax.broadcasted_iota(jnp.int32, shape, 1)
    full = jnp.where(source // sz.lev == target // sz.lev, full, 0.0)
    stay = 1.0 - 2.0 * DIFFUSE_ALONG - 2.0 * DIFFUSE_ACROSS
    full = full + jnp.where(source == target, stay, 0.0)
    coarse = full.astype(jnp.bfloat16)
    fine = (full - coarse.astype(jnp.float32)).astype(jnp.bfloat16)
    w_ref[0 : sz.lanes, 0 : sz.lanes] = coarse
    w_ref[sz.lanes :, 0 : sz.lanes] = coarse
    w_ref[0 : sz.lanes, sz.lanes :] = fine
    w_ref[sz.lanes :, sz.lanes :] = fine


def combine(count, packet, *refs):
    own, zfirst, zlast = refs[:3]
    parts = refs[3 : 3 + count]
    total_ref, first_ref, last_ref = refs[3 + count :]
    total = own[0 : 2 * packet, :]
    for part in parts:
        total = total + part[0 : 2 * packet, :]
    total_ref[...] = total
    first_ref[0 : 2 * packet, :] = total
    first_ref[2 * packet :, :] = zfirst[...]
    last_ref[0 : 2 * packet, :] = total
    last_ref[2 * packet :, :] = zlast[...]


def substeps(sz, w_ref, a_ref, b_ref, ca_ref, cb_ref, courant_ref):
    lo_y = PAD * sz.group
    rows = (sz.half + 2 * SUB) * sz.group
    c = courant_ref[lo_y : lo_y + rows, :]
    ca_ref[lo_y : lo_y + rows, :] = DIFFUSE_ALONG - 0.5 * c
    cb_ref[lo_y : lo_y + rows, :] = DIFFUSE_ALONG + 0.5 * c
    g = sz.group

    def step(src, dst):
        total = sz.half + 2 * SUB - 2
        for begin in range(0, total, CHUNK):
            size = min(CHUNK, total - begin)
            y = PAD + 1 + begin
            n = size * g
            here = [src[(w * sz.span + y) * g : (w * sz.span + y) * g + n, :] for w in range(sz.wid)]
            stacked = jnp.concatenate(here, axis=0)
            coarse = stacked.astype(jnp.bfloat16)
            fine = (stacked - coarse.astype(jnp.float32)).astype(jnp.bfloat16)
            product = jnp.dot(
                jnp.concatenate([coarse, fine], axis=1), w_ref[...],
                preferred_element_type=jnp.float32,
            )
            ca = ca_ref[y * g : y * g + n, :]
            cb = cb_ref[y * g : y * g + n, :]
            for w in range(sz.wid):
                at = (w * sz.span + y) * g
                up = here[min(w + 1, sz.wid - 1)]
                down = here[max(w - 1, 0)]
                part = product[w * n : (w + 1) * n]
                value = part[:, : sz.lanes] + part[:, sz.lanes :]
                value = value + DIFFUSE_ACROSS * (up + down)
                value = value + src[at + g : at + g + n, :] * ca
                value = value + src[at - g : at - g + n, :] * cb
                dst[at : at + n, :] = value

    def pair(_, carry):
        step(a_ref, b_ref)
        step(b_ref, a_ref)
        return carry

    lax.fori_loop(0, SUB // 2, pair, 0)


def merid_kernel(sz, lat_two, place, mt, mct, w_ref, pole, lat_a, lat_b, own_b, out_ref,
                 b_ref, ca_ref, cb_ref, ct_ref):
    lat = place[1]
    last = place[2]
    out_ref[...] = mt[...]
    ct_ref[...] = mct[...]
    base = 2 * sz.packet
    for d in range(SUB):
        for slot in range(sz.packed):
            courant = slot >= sz.wr
            w, r = divmod(slot, sz.rows)
            partner = slot if courant else (sz.wid - 1 - w) * sz.rows + r
            sign = -1.0 if courant else 1.0
            ref = ct_ref if courant else out_ref
            begin = 0 if courant else w * sz.span
            mirrored = (SUB - 1 - d) * sz.packed + partner
            over = sign * pole[base + mirrored : base + mirrored + 1, :]
            at = d * sz.packed + slot
            south = jnp.where(lat == 0, over, lat_a[at : at + 1, :])
            north = jnp.where(lat == last, over, lat_b[at : at + 1, :])
            row = (begin + PAD + d) * sz.group + r
            ref[row : row + 1, :] = south
            row = (begin + PAD + SUB + sz.half + d) * sz.group + sz.rows + r
            ref[row : row + 1, :] = north
    substeps(sz, w_ref, out_ref, b_ref, ca_ref, cb_ref, ct_ref)


def zonal_kernel(sz, shift_count, place, length, zt, zct, w_ref, owner, own, behind, ahead, *refs):
    others = refs[:shift_count]
    out_ref, near_ref, b_ref, ca_ref, cb_ref, ct_ref = refs[shift_count:]
    lon = place[0]
    out_ref[...] = zt[...]
    ct_ref[...] = zct[...]
    ends = own[...] + behind[0 : 2 * sz.packet, :] + ahead[0 : 2 * sz.packet, :]
    for other in others:
        ends = ends + other[...]
    head = ends[: sz.packet]
    left = jnp.where(lon == 0, ends[sz.packet :], behind[2 * sz.packet :, :])
    right = ahead[2 * sz.packet :, :]
    for d in range(SUB):
        for slot in range(sz.packed):
            courant = slot >= sz.wr
            w, r = divmod(slot, sz.rows)
            ref = ct_ref if courant else out_ref
            r = slot % sz.rows
            begin = 0 if courant else w * sz.span
            at = d * sz.packed + slot
            row = (begin + PAD + d) * sz.group + r
            ref[row : row + 1, :] = left[at : at + 1]
            row = (begin + PAD + SUB + sz.half + d) * sz.group + sz.rows + r
            ref[row : row + 1, :] = right[at : at + 1]
    for r in range(sz.rows):
        past = length[r] - lon * sz.cells
        for h in range(2):
            y = jnp.clip(past + PAD + SUB - h * sz.half, 0, sz.span - SUB)
            for slot in range(r, sz.packed, sz.rows):
                courant = slot >= sz.wr
                ref = ct_ref if courant else out_ref
                begin = 0 if courant else (slot // sz.rows) * sz.span
                for d in range(SUB):
                    at = d * sz.packed + slot
                    row = (begin + y + d) * sz.group + h * sz.rows + r
                    ref[pl.ds(row, 1), :] = head[at : at + 1]
    substeps(sz, w_ref, out_ref, b_ref, ca_ref, cb_ref, ct_ref)
    scale = GLON_DEV / (3.0 * CELLS_DEV)
    near = near_ref.shape[0] // sz.rows
    for r in range(sz.rows):
        column = lon * GLON_DEV - 1 + lax.broadcasted_iota(jnp.int32, (near, sz.cells), 0)
        cell = lon * sz.cells + lax.broadcasted_iota(jnp.int32, (near, sz.cells), 1)
        own_row = owner[r : r + 1, :]
        table = jnp.where((own_row == column) & (cell < length[r]), 1.0, 0.0)
        halves = []
        for h in range(2):
            change = None
            for w in range(sz.wid):
                at = pl.ds((w * sz.span + PAD + SUB) * sz.group + h * sz.rows + r,
                           sz.half, stride=sz.group)
                part = out_ref[at, :] - zt[at, :]
                change = part if change is None else change + part
            halves.append(change)
        change = jnp.concatenate(halves, axis=0) * scale
        near_ref[pl.ds(r, near, stride=sz.rows), :] = jnp.dot(
            table.astype(jnp.float32), change, precision=lax.Precision.HIGHEST,
            preferred_element_type=jnp.float32,
        )


def turn_out(sz, place, length, mt, zt, z_ref, m_out, z_out):
    lon = place[0]
    cell = lon * sz.cells + lax.broadcasted_iota(jnp.int32, (sz.lanes, sz.cells), 1)
    for zonal, src, dst in ((False, mt, m_out), (True, zt, z_out)):
        for w in range(sz.wid):
            for r in range(sz.rows):
                halves = [
                    src[pl.ds((w * sz.span + PAD + SUB) * sz.group + h * sz.rows + r,
                              sz.half, stride=sz.group), :]
                    for h in range(2)
                ]
                value = jnp.concatenate(halves, axis=0).T
                at = pl.ds(w * sz.rows + r, sz.lanes, stride=sz.wr)
                if zonal:
                    value = jnp.where(cell < length[r], value, z_ref[at, :])
                dst[at, :] = value


def call(body, outs, smem, vmem, scratch=(), name=None):
    return pl.pallas_call(
        body,
        out_shape=outs,
        in_specs=[pl.BlockSpec(memory_space=pltpu.SMEM)] * smem
        + [pl.BlockSpec(memory_space=pltpu.VMEM)] * vmem,
        out_specs=[pl.BlockSpec(memory_space=pltpu.VMEM)] * len(outs),
        scratch_shapes=list(scratch),
        name=name,
    )


def shifted(value, axis, steps):
    count = lax.axis_size(axis)
    return lax.ppermute(value, axis, [(i, (i + steps) % count) for i in range(count)])


def shards(
    zonal_state, zonal_courant, zonal_length, zonal_owner, merid_state, merid_courant, mixing
):
    sz = Sizes(zonal_state.shape)
    f32 = lambda *shape: jax.ShapeDtypeStruct(shape, jnp.float32)
    lon_count = lax.axis_size("lon")
    lat_count = lax.axis_size("lat")
    lat_two = lat_count == 2
    place = jnp.stack(
        [lax.axis_index("lon"), lax.axis_index("lat"), jnp.int32(lat_count - 1)]
    ).astype(jnp.int32)
    flat = lambda a: a.reshape(-1, sz.cells)
    z, m = flat(zonal_state), flat(merid_state)
    state_rows = sz.wid * sz.span * sz.group
    courant_rows = sz.span * sz.group
    packet = sz.packet
    lanes = sz.lanes
    zt, zct, mt, mct, weights, zfirst, zlast, ht, htp, mlow, mhigh = call(
        functools.partial(turn_in, sz, lat_two),
        (
            f32(state_rows, lanes), f32(courant_rows, lanes),
            f32(state_rows, lanes), f32(courant_rows, lanes),
            jax.ShapeDtypeStruct((2 * lanes, 2 * lanes), jnp.bfloat16),
            f32(packet, lanes), f32(packet, lanes), f32(2 * packet, lanes),
            f32(3 * packet, lanes), f32(packet, lanes), f32(packet, lanes),
        ),
        2, 5,
        (
            pltpu.VMEM((sz.cells + 16, lanes), jnp.float32),
            pltpu.VMEM((packet, lanes), jnp.float32),
            pltpu.VMEM((packet, lanes), jnp.float32),
        ),
        "turn_in",
    )(place, zonal_length, z, flat(zonal_courant), m, flat(merid_courant),
      mixing.reshape(lanes, sz.lev))
    pole = shifted(htp, "lon", lon_count // 2)
    if lat_two:
        lat_a = lat_b = shifted(mlow, "lat", 1)
    else:
        lat_b = shifted(mlow, "lat", -1)
        lat_a = shifted(mhigh, "lat", 1)
    stride = lon_count
    own = ht
    stages = []
    while stride > 4:
        radix = 4 if stride % 16 == 0 and stride != lon_count * 2 else 2
        stages.append((stride // radix, radix))
        stride //= radix
    for number, (width, radix) in enumerate(stages):
        parts = []
        for s in range(1, radix):
            if number == 0 and s * width == lon_count // 2:
                parts.append(pole)
            else:
                parts.append(shifted(own, "lon", s * width))
        own, to_left, to_right = call(
            functools.partial(combine, len(parts), packet),
            (f32(2 * packet, lanes), f32(3 * packet, lanes), f32(3 * packet, lanes)),
            0, 3 + len(parts), (), "combine",
        )(own, zfirst, zlast, *parts)
    behind = shifted(to_right, "lon", 1)
    ahead = shifted(to_left, "lon", -1)
    others = [shifted(own, "lon", s) for s in range(2, stride - 1)]
    work = (
        pltpu.VMEM((state_rows, lanes), jnp.float32),
        pltpu.VMEM((courant_rows, lanes), jnp.float32),
        pltpu.VMEM((courant_rows, lanes), jnp.float32),
        pltpu.VMEM((courant_rows, lanes), jnp.float32),
    )
    (mt_next,) = call(
        functools.partial(merid_kernel, sz, lat_two),
        (f32(state_rows, lanes),), 1, 7, work, "merid",
    )(place, mt, mct, weights, pole, lat_a, lat_b, mhigh)
    near = 8
    zt_next, near_terms = call(
        functools.partial(zonal_kernel, sz, len(others)),
        (f32(state_rows, lanes), f32(near * sz.rows, lanes)), 2, 7 + len(others), work, "zonal",
    )(place, zonal_length, zt, zct, weights, zonal_owner, own, behind, ahead, *others)
    near_terms = near_terms.reshape(near, sz.rows, lanes)
    from_right = shifted(near_terms[0], "lon", -1)
    from_left = shifted(near_terms[GLON_DEV + 1], "lon", 1)
    m_next, z_next = call(
        functools.partial(turn_out, sz),
        (f32(*m.shape), f32(*z.shape)), 2, 3, (), "turn_out",
    )(place, zonal_length, mt_next, zt_next, z)
    coupling = near_terms[1 : GLON_DEV + 1]
    coupling = jnp.concatenate(
        [coupling[:1] + from_left[None], coupling[1:-1], coupling[-1:] + from_right[None]]
    )
    return z_next.reshape(zonal_state.shape), m_next.reshape(merid_state.shape), coupling


def solution(mesh):
    return jax.shard_map(
        shards,
        mesh=mesh,
        in_specs=(
            P(None, None, None, "lat", "lon"),
            P(None, "lat", "lon"),
            P("lat"),
            P("lat", "lon"),
            P(None, None, None, "lon", "lat"),
            P(None, "lon", "lat"),
            P(),
        ),
        out_specs=(
            P(None, None, None, "lat", "lon"),
            P(None, None, None, "lon", "lat"),
            P("lon", "lat", None),
        ),
        check_vma=False,
    )
```

time: 468 us -> 53.3 us (0.11); the launches traced: 459 us -> 52.9 us
  blocking collectives: 234 us -> 0 us
  local copies, waits for them, and re-layouts: 106 us -> 3.34 us
  other arithmetic: 38.5 us -> 2.66 us
  starting transfers between devices: 47.3 us -> 14.1 us
  matrix products: 25.9 us -> 0 us
  Pallas kernels: 0 us -> 17.3 us
  waiting for transfers between devices: 6.03 us -> 14.9 us
    psum x4 -> x0, blocking collectives: 234 us -> none  [cycle_ends(): return lax.psum((head_part, tail_part), 'lon')]
    ppermute x22 -> x9, starting transfers between devices: 47.3 us -> 14.1 us  [shifted(): lax.ppermute(value, axis, [(i, (i + steps) % count) for i in range(count)])]
    slice x37 -> x2, local copies, waits for them, and re-layouts: 34.1 us -> 1.36 us  [the longest x1 0.69 us: shards(): from_left = shifted(near_terms[GLON_DEV + 1], 'lon', 1)]
    scatter x8 -> x0, local copies, waits for them, and re-layouts: 29.9 us -> none  [the longest x4 21.8 us: shards(): forward_side.at[..., -1]]
    dot_general x9 -> x0, matrix products: 25.9 us -> none  [the longest x8 25.6 us: tendency(): jnp.einsum('vkj,vjwrx->vkwrx', mixing, field_now, precision=lax.Precision...]
    ppermute x10 -> x0, local copies, waits for them, and re-layouts: 18.3 us -> none  [the longest x5 9.15 us: padded_2(): lax.ppermute(tail, axis, [(i, (i + 1) % count) for i in range(ends)])]
    pallas_call x0 -> x5, Pallas kernels: none -> 17.3 us  [the longest x1 4.41 us: shards(): call(functools.partial(zonal_kernel, sz, len(others)), (f32(state_rows, l...]
    concatenate x5 -> x1, other arithmetic: 13.2 us -> 0.6 us  [shards(): jnp.concatenate([coupling[:1] + from_left[None], coupling[1:-1], coupling...]
  transfers between devices with their start and end apart: 22 -> 9, of which waited for: 4 -> 4; matrix products, arithmetic and copies ran while one was open for 36% -> 3% of each run, Pallas kernels for 0% -> 14%
where the time goes in v1:
time: 53.3 us; the launch traced here: 52.9 us
  Pallas kernels  17.3 us (32%)
  waiting for transfers between devices  14.9 us (28%)
  starting transfers between devices  14.1 us (26%)
  local copies, waits for them, and re-layouts  3.34 us (6%)
  other arithmetic  2.66 us (5%)
  between operations  0.67 us (1%)
    ppermute x9, waiting for transfers between devices, shifted(): lax.ppermute(value, axis, [(i, (i + steps) % count) for i in range(count)])  14.9 us
    ppermute x9, starting transfers between devices, shifted(): lax.ppermute(value, axis, [(i, (i + steps) % count) for i in range(count)])  14.1 us
    pallas_call x1, Pallas kernels, shards(): call(functools.partial(zonal_kernel, sz, len(others)), (f32(state_rows, l...  4.41 us
    pallas_call x1, Pallas kernels, shards(): call(functools.partial(merid_kernel, sz, lat_two), (f32(state_rows, lanes...  4.23 us
    pallas_call x1, Pallas kernels, shards(): call(functools.partial(turn_in, sz, lat_two), (f32(state_rows, lanes), f3...  3.83 us
    pallas_call x1, Pallas kernels, shards(): call(functools.partial(turn_out, sz), (f32(*m.shape), f32(*z.shape)), 2,...  3.14 us
    unnamed x16, local copies, waits for them, and re-layouts  1.98 us
    pallas_call x1, Pallas kernels, shards(): call(functools.partial(combine, len(parts), packet), (f32(2 * packet, lan...  1.72 us
  transfers between devices with their start and end apart: 9, of which 4 were waited for; matrix products, arithmetic and copies ran while one was open for 3% of the time, Pallas kernels for 14%

profile of v1, /device:TPU:0, one launch (start us, length us, event | category | flops | bytes accessed | tf_op | source)
XLA Modules:
  0.0 52.9 jit_solution(14665671510973528812)
XLA Ops:
  0.6 0.6 %pad_add_fusion.place = s32[3]{0:T(128)} fusion(s32[1]{0:T(128)} %constant.9.clone.1, s32[1]{0:T(128)} %bitcast.1, s32[1]{0:T(128)} %bitcast), kind=kLoop, calls=%fused_computation.3 | loop fusion | flops 6 | bytes 24 | tf_op jit(solution)/shard_map/stack | solution.py:297
  1.3 3.8 %turn_in.1 = (f32[1920,128]{1,0:T(8,128)}, f32[640,128]{1,0:T(8,128)}, f32[1920,128]{1,0:T(8,128)}, f32[640,128]{1,0:T(8,128)}, bf16[256,256]{1,0:T(8,128)(2,1)}...) custom-call(s32[3]{0:T(128)} %pad_add_fusion.place, ...), custom_call_target="tpu_custom_call" | custom-call | tf_op jit(solution)/shard_map/turn_in/pallas_call | solution.py:306
  5.1 4.1 %collective-permute-start = (f32[192,128]{1,0:T(8,128)}, f32[192,128]{1,0:T(8,128)S(1)}, u32[]{:S(2)}, u32[]{:S(2)}) collective-permute-start(f32[192,128]{1,0:T(8,128)} %get-tuple-element.24), channel_id=1, source_target_pairs={{0,16},{2,18},{4,20},{6,22},{8,24},{10,26},{12,28},{14,30},{16,0},... | collective-permute-start | bytes 294920 | tf_op jit(solution)/shard_map/ppermute | solution.py:286
  9.2 1.6 %collective-permute-start.2 = (f32[128,128]{1,0:T(8,128)}, f32[128,128]{1,0:T(8,128)S(1)}, u32[]{:S(2)}, u32[]{:S(2)}) collective-permute-start(f32[128,128]{1,0:T(8,128)} %get-tuple-element.29.refs_0_), channel_id=1, source_target_pairs={{0,8},{2,10},{4,12},{6,14},{8,16},{10,18},{12,20},{14,22},{16,24},... | collective-permute-start | bytes 196616 | tf_op jit(solution)/shard_map/ppermute | solution.py:286
  10.8 2.2 %collective-permute-start.3 = (f32[128,128]{1,0:T(8,128)}, f32[128,128]{1,0:T(8,128)S(1)}, u32[]{:S(2)}, u32[]{:S(2)}) collective-permute-start(f32[128,128]{1,0:T(8,128)} %get-tuple-element.29.refs_0_), channel_id=1, source_target_pairs={{0,24},{2,26},{4,28},{6,30},{8,0},{10,2},{12,4},{14,6},{16,8},{18,... | collective-permute-start | bytes 196616 | tf_op jit(solution)/shard_map/ppermute | solution.py:286
  13.0 2.6 %collective-permute-done.2.refs_3_ = f32[128,128]{1,0:T(8,128)S(1)} collective-permute-done((f32[128,128]{1,0:T(8,128)}, f32[128,128]{1,0:T(8,128)S(1)}, u32[]{:S(2)}, u32[]{:S(2)}) %collective-permute-start.2) | collective-permute-done | bytes 65568 | tf_op jit(solution)/shard_map/ppermute | solution.py:286
  15.6 1.0 %collective-permute-done.3.refs_5_ = f32[128,128]{1,0:T(8,128)S(1)} collective-permute-done((f32[128,128]{1,0:T(8,128)}, f32[128,128]{1,0:T(8,128)S(1)}, u32[]{:S(2)}, u32[]{:S(2)}) %collective-permute-start.3) | collective-permute-done | bytes 65568 | tf_op jit(solution)/shard_map/ppermute | solution.py:286
  16.6 0.0 collective-permute-done.pole.refs_4_
  16.6 0.6 %copy-done.5 = f32[128,128]{1,0:T(8,128)} copy-done((f32[128,128]{1,0:T(8,128)}, f32[128,128]{1,0:T(8,128)S(1)}, u32[]{:S(2)}) %copy-start.5) | copy-done | bytes 65560
  17.2 0.1 copy-done
  17.3 1.7 %combine.1 = (f32[128,128]{1,0:T(8,128)}, f32[192,128]{1,0:T(8,128)}, f32[192,128]{1,0:T(8,128)}) custom-call(f32[128,128]{1,0:T(8,128)} %get-tuple-element.29.refs_0_, f32[64,128]{1,0:T(8,128)} %get-tuple-element.30.refs_1_, f32[64,128]{1,0:T(8,128)} %get-tuple-element.31.refs_2_, f32[128,128]{1,0:T(8,128)} %copy-done.4, f32[192,128]{1,0:T(8,128)} %copy-done, ...), custom_call_target="tpu_custom_call" | custom-call | tf_op jit(solution)/shard_map/combine/pallas_call | solution.py:344
  19.0 0.0 collective-permute-start.4
  19.0 4.4 %collective-permute-start.5 = (f32[192,128]{1,0:T(8,128)}, f32[192,128]{1,0:T(8,128)S(1)}, u32[]{:S(2)}, u32[]{:S(2)}) collective-permute-start(f32[192,128]{1,0:T(8,128)} %get-tuple-element.34), channel_id=1, source_target_pairs={{0,30},{2,0},{4,2},{6,4},{8,6},{10,8},{12,10},{14,12},{16,14},{18,... | collective-permute-start | bytes 294920 | tf_op jit(solution)/shard_map/ppermute | solution.py:286
  23.4 0.0 collective-permute-start.6
  23.4 7.2 %collective-permute-done.6.refs_0_ = f32[128,128]{1,0:T(8,128)S(1)} collective-permute-done((f32[128,128]{1,0:T(8,128)}, f32[128,128]{1,0:T(8,128)S(1)}, u32[]{:S(2)}, u32[]{:S(2)}) %collective-permute-start.6) | collective-permute-done | bytes 65568 | tf_op jit(solution)/shard_map/ppermute | solution.py:286
  30.6 0.6 %copy-done.6 = f32[128,128]{1,0:T(8,128)} copy-done((f32[128,128]{1,0:T(8,128)}, f32[128,128]{1,0:T(8,128)S(1)}, u32[]{:S(2)}) %copy-start.6) | copy-done | bytes 65560
  31.2 0.0 copy-done.2
  31.3 0.1 copy-done.3
  31.3 4.4 %zonal.1 = (f32[1920,128]{1,0:T(8,128)}, f32[32,128]{1,0:T(8,128)}) custom-call(s32[3]{0:T(128)} %pad_add_fusion.place, s32[4]{0:T(128)} %length.5, f32[1920,128]{1,0:T(8,128)} %get-tuple-element.27.zt, f32[640,128]{1,0:T(8,128)} %get-tuple-element.28.zct, bf16[256,256]{1,0:T(8,128)(2,1)} %get-tuple-element.23.w_ref, s32[4,128]{1,0:T(4,128)} %owner.1, ...), custom_call_target="tpu_custom_call" | custom-call | tf_op jit(solution)/shard_map/zonal/pallas_call | solution.py:363
  35.8 0.7 %slice.28 = f32[4,128]{1,0:T(4,128)S(1)} slice(f32[32,128]{1,0:T(8,128)} %get-tuple-element.38), slice={[20:24], [0:128]} | slice | bytes 4096 | tf_op jit(solution)/shard_map/slice | solution.py:369
  36.4 0.0 collective-permute-start.7
  36.4 1.6 %collective-permute-start.1 = (f32[64,128]{1,0:T(8,128)S(1)}, f32[64,128]{1,0:T(8,128)S(1)}, u32[]{:S(2)}, u32[]{:S(2)}) collective-permute-start(f32[64,128]{1,0:T(8,128)S(1)} %copy-done.7), channel_id=1, source_target_pairs={{0,1},{1,0},{2,3},{3,2},{4,5},{5,4},{6,7},{7,6},{8,9},{9,8},{10,11... | collective-permute-start | bytes 98312 | tf_op jit(solution)/shard_map/ppermute | solution.py:286
  38.1 4.1 %collective-permute-done.7 = f32[4,128]{1,0:T(4,128)S(1)} collective-permute-done((f32[4,128]{1,0:T(4,128)S(1)}, f32[4,128]{1,0:T(4,128)S(1)}, u32[]{:S(2)}, u32[]{:S(2)}) %collective-permute-start.7) | collective-permute-done | bytes 2080 | tf_op jit(solution)/shard_map/ppermute | solution.py:286
  42.1 0.7 %add_bitcast_fusion.1 = (f32[1,4,128]{2,1,0:T(4,128)S(1)}, f32[4,128]{1,0:T(4,128)S(1)}) fusion(f32[4,128]{1,0:T(4,128)S(1)} %collective-permute-done.7, f32[32,128]{1,0:T(8,128)} %get-tuple-element.38), kind=kLoop, calls=%fused_computation.2 | loop fusion | flops 512 | bytes 10240 | tf_op jit(solution)/shard_map/add | solution.py:376
  42.9 0.1 collective-permute-start.8
  43.0 0.0 collective-permute-done.1.lat_a.lat_b
  43.0 0.6 %copy-done.1 = f32[64,128]{1,0:T(8,128)} copy-done((f32[64,128]{1,0:T(8,128)}, f32[64,128]{1,0:T(8,128)S(1)}, u32[]{:S(2)}) %copy-start.1) | copy-done | bytes 32792
  43.6 4.2 %merid.1.mt = f32[1920,128]{1,0:T(8,128)} custom-call(s32[3]{0:T(128)} %pad_add_fusion.place, f32[1920,128]{1,0:T(8,128)} %get-tuple-element.21.mt, f32[640,128]{1,0:T(8,128)} %get-tuple-element.22.mct, bf16[256,256]{1,0:T(8,128)(2,1)} %get-tuple-element.23.w_ref, f32[192,128]{1,0:T(8,128)} %copy-done, f32[64,128]{1,0:T(8,128)} %copy-done.1, ...), custom_call_target="tpu_custom_call" | custom-call | tf_op jit(solution)/shard_map/merid/pallas_call | solution.py:358
  47.8 0.7 %slice.29 = f32[8,128]{1,0:T(8,128)S(1)} slice(f32[32,128]{1,0:T(8,128)} %get-tuple-element.38), slice={[8:16], [0:128]} | slice | bytes 8192 | tf_op jit(solution)/shard_map/slice | solution.py:376
  48.5 3.1 %turn_out.1 = (f32[1536,128]{1,0:T(8,128)}, f32[1536,128]{1,0:T(8,128)}) custom-call(s32[3]{0:T(128)} %pad_add_fusion.place, s32[4]{0:T(128)} %length.5, f32[1920,128]{1,0:T(8,128)} %merid.1.mt, f32[1920,128]{1,0:T(8,128)} %get-tuple-element.35.zt, f32[1536,128]{1,0:T(8,128)} %bitcast.15), custom_call_target="tpu_custom_call" | custom-call | tf_op jit(solution)/shard_map/turn_out/pallas_call | solution.py:370
  51.6 0.7 %add_bitcast_fusion = f32[1,4,128]{2,1,0:T(4,128)S(1)} fusion(f32[4,128]{1,0:T(4,128)S(1)} %collective-permute-done.8, f32[32,128]{1,0:T(8,128)} %get-tuple-element.38), kind=kLoop, calls=%fused_computation.1 | loop fusion | flops 512 | bytes 6144 | tf_op jit(solution)/shard_map/add | solution.py:376
  52.3 0.6 %pad_maximum_fusion = f32[4,4,128]{2,1,0:T(4,128)} fusion(f32[1,4,128]{2,1,0:T(4,128)S(1)} %add_bitcast_fusion, f32[2,4,128]{2,1,0:T(4,128)S(1)} %bitcast.20, f32[1,4,128]{2,1,0:T(4,128)S(1)} %get-tuple-element.39), kind=kLoop, calls=%fused_computation | loop fusion | flops 4096 | bytes 16384 | tf_op jit(solution)/shard_map/concatenate | solution.py:375
  (13 shorter events, 0.0 us)
Async XLA Ops:
  5.1 11.5 %collective-permute-start = (f32[192,128]{1,0:T(8,128)}, f32[192,128]{1,0:T(8,128)S(1)}, u32[]{:S(2)}, u32[]{:S(2)}) collective-permute-start(f32[192,128]{1,0:T(8,128)} %get-tuple-element.24), channel_id=1, source_target_pairs={{0,16},{2,18},{4,20},{6,22},{8,24},{10,26},{12,28},{14,30},{16,0},... | collective-permute-start | bytes 294920 | tf_op jit(solution)/shard_map/ppermute | solution.py:286
  9.2 6.4 %collective-permute-start.2 = (f32[128,128]{1,0:T(8,128)}, f32[128,128]{1,0:T(8,128)S(1)}, u32[]{:S(2)}, u32[]{:S(2)}) collective-permute-start(f32[128,128]{1,0:T(8,128)} %get-tuple-element.29.refs_0_), channel_id=1, source_target_pairs={{0,8},{2,10},{4,12},{6,14},{8,16},{10,18},{12,20},{14,22},{16,24},... | collective-permute-start | bytes 196616 | tf_op jit(solution)/shard_map/ppermute | solution.py:286
  10.8 5.8 %collective-permute-start.3 = (f32[128,128]{1,0:T(8,128)}, f32[128,128]{1,0:T(8,128)S(1)}, u32[]{:S(2)}, u32[]{:S(2)}) collective-permute-start(f32[128,128]{1,0:T(8,128)} %get-tuple-element.29.refs_0_), channel_id=1, source_target_pairs={{0,24},{2,26},{4,28},{6,30},{8,0},{10,2},{12,4},{14,6},{16,8},{18,... | collective-permute-start | bytes 196616 | tf_op jit(solution)/shard_map/ppermute | solution.py:286
  15.6 1.0 %copy-start.4 = (f32[128,128]{1,0:T(8,128)}, f32[128,128]{1,0:T(8,128)S(1)}, u32[]{:S(2)}) copy-start(f32[128,128]{1,0:T(8,128)S(1)} %collective-permute-done.2.refs_3_) | copy-start | bytes 196612
  16.6 0.6 %copy-start.5 = (f32[128,128]{1,0:T(8,128)}, f32[128,128]{1,0:T(8,128)S(1)}, u32[]{:S(2)}) copy-start(f32[128,128]{1,0:T(8,128)S(1)} %collective-permute-done.3.refs_5_) | copy-start | bytes 196612
  16.6 0.7 %copy-start = (f32[192,128]{1,0:T(8,128)}, f32[192,128]{1,0:T(8,128)S(1)}, u32[]{:S(2)}) copy-start(f32[192,128]{1,0:T(8,128)S(1)} %collective-permute-done.pole.refs_4_) | copy-start | bytes 294916
  19.0 11.6 %collective-permute-start.4 = (f32[192,128]{1,0:T(8,128)}, f32[192,128]{1,0:T(8,128)S(1)}, u32[]{:S(2)}, u32[]{:S(2)}) collective-permute-start(f32[192,128]{1,0:T(8,128)} %get-tuple-element.33), channel_id=1, source_target_pairs={{0,2},{2,4},{4,6},{6,8},{8,10},{10,12},{12,14},{14,16},{16,18},{18... | collective-permute-start | bytes 294920 | tf_op jit(solution)/shard_map/ppermute | solution.py:286
  19.0 11.6 %collective-permute-start.5 = (f32[192,128]{1,0:T(8,128)}, f32[192,128]{1,0:T(8,128)S(1)}, u32[]{:S(2)}, u32[]{:S(2)}) collective-permute-start(f32[192,128]{1,0:T(8,128)} %get-tuple-element.34), channel_id=1, source_target_pairs={{0,30},{2,0},{4,2},{6,4},{8,6},{10,8},{12,10},{14,12},{16,14},{18,... | collective-permute-start | bytes 294920 | tf_op jit(solution)/shard_map/ppermute | solution.py:286
  23.4 7.2 %collective-permute-start.6 = (f32[128,128]{1,0:T(8,128)}, f32[128,128]{1,0:T(8,128)S(1)}, u32[]{:S(2)}, u32[]{:S(2)}) collective-permute-start(f32[128,128]{1,0:T(8,128)} %get-tuple-element.32.own), channel_id=1, source_target_pairs={{0,4},{2,6},{4,8},{6,10},{8,12},{10,14},{12,16},{14,18},{16,20},{1... | collective-permute-start | bytes 196616 | tf_op jit(solution)/shard_map/ppermute | solution.py:286
  30.6 0.6 %copy-start.6 = (f32[128,128]{1,0:T(8,128)}, f32[128,128]{1,0:T(8,128)S(1)}, u32[]{:S(2)}) copy-start(f32[128,128]{1,0:T(8,128)S(1)} %collective-permute-done.6.refs_0_) | copy-start | bytes 196612
  30.6 0.7 %copy-start.2 = (f32[192,128]{1,0:T(8,128)}, f32[192,128]{1,0:T(8,128)S(1)}, u32[]{:S(2)}) copy-start(f32[192,128]{1,0:T(8,128)S(1)} %collective-permute-done.4.behind) | copy-start | bytes 294916
  30.6 0.7 %copy-start.3 = (f32[192,128]{1,0:T(8,128)}, f32[192,128]{1,0:T(8,128)S(1)}, u32[]{:S(2)}) copy-start(f32[192,128]{1,0:T(8,128)S(1)} %collective-permute-done.5.ahead) | copy-start | bytes 294916
  31.3 5.1 %copy-start.7 = (f32[64,128]{1,0:T(8,128)S(1)}, f32[64,128]{1,0:T(8,128)}, u32[]{:S(2)}) copy-start(f32[64,128]{1,0:T(8,128)} %get-tuple-element.25) | copy-start | bytes 98308
  36.4 5.7 %collective-permute-start.7 = (f32[4,128]{1,0:T(4,128)S(1)}, f32[4,128]{1,0:T(4,128)S(1)}, u32[]{:S(2)}, u32[]{:S(2)}) collective-permute-start(f32[4,128]{1,0:T(4,128)S(1)} %slice.28), channel_id=1, source_target_pairs={{0,2},{2,4},{4,6},{6,8},{8,10},{10,12},{12,14},{14,16},{16,18},{18... | collective-permute-start | bytes 6152 | tf_op jit(solution)/shard_map/ppermute | solution.py:286
  36.4 6.5 %collective-permute-start.1 = (f32[64,128]{1,0:T(8,128)S(1)}, f32[64,128]{1,0:T(8,128)S(1)}, u32[]{:S(2)}, u32[]{:S(2)}) collective-permute-start(f32[64,128]{1,0:T(8,128)S(1)} %copy-done.7), channel_id=1, source_target_pairs={{0,1},{1,0},{2,3},{3,2},{4,5},{5,4},{6,7},{7,6},{8,9},{9,8},{10,11... | collective-permute-start | bytes 98312 | tf_op jit(solution)/shard_map/ppermute | solution.py:286
  42.9 8.7 %collective-permute-start.8 = (f32[4,128]{1,0:T(4,128)S(1)}, f32[4,128]{1,0:T(4,128)S(1)}, u32[]{:S(2)}, u32[]{:S(2)}) collective-permute-start(f32[4,128]{1,0:T(4,128)S(1)} %get-tuple-element.40), channel_id=1, source_target_pairs={{0,30},{2,0},{4,2},{6,4},{8,6},{10,8},{12,10},{14,12},{16,14},{18,... | collective-permute-start | bytes 6152 | tf_op jit(solution)/shard_map/ppermute | solution.py:286
  43.0 0.6 %copy-start.1 = (f32[64,128]{1,0:T(8,128)}, f32[64,128]{1,0:T(8,128)S(1)}, u32[]{:S(2)}) copy-start(f32[64,128]{1,0:T(8,128)S(1)} %collective-permute-done.1.lat_a.lat_b) | copy-start | bytes 98308

commit v2 on v1

--- a/solution.py
+++ b/solution.py
@@ -14,6 +14,7 @@
 DIFFUSE_ACROSS = 0.1
 PAD = 4
 CHUNK = 10
+VMEM_GRANT = 12 << 20
 
 
 class Sizes:
@@ -43,12 +44,12 @@
     ]
 
 
-def turn_in(sz, lat_two, place, length, z_ref, zc_ref, m_ref, mc_ref, mix_ref,
+def turn_in(sz, lat_two, lat_count, length, z_ref, zc_ref, m_ref, mc_ref, mix_ref,
             zt_ref, zct_ref, mt_ref, mct_ref, w_ref, zfirst, zlast, ht, htp, mlow, mhigh,
             tile, low, high):
-    lon = place[0]
-    lat = place[1]
-    last = place[2]
+    lon = lax.axis_index("lon")
+    lat = lax.axis_index("lat")
+    last = lat_count - 1
     edge = 8
     tile[0:edge, :] = jnp.zeros((edge, sz.lanes), jnp.float32)
     tile[edge + sz.cells :, :] = jnp.zeros((edge, sz.lanes), jnp.float32)
@@ -164,10 +165,10 @@
     lax.fori_loop(0, SUB // 2, pair, 0)
 
 
-def merid_kernel(sz, lat_two, place, mt, mct, w_ref, pole, lat_a, lat_b, own_b, out_ref,
+def merid_kernel(sz, lat_two, lat_count, mt, mct, w_ref, pole, lat_a, lat_b, own_b, out_ref,
                  b_ref, ca_ref, cb_ref, ct_ref):
-    lat = place[1]
-    last = place[2]
+    lat = lax.axis_index("lat")
+    last = lat_count - 1
     out_ref[...] = mt[...]
     ct_ref[...] = mct[...]
     base = 2 * sz.packet
@@ -191,10 +192,10 @@
     substeps(sz, w_ref, out_ref, b_ref, ca_ref, cb_ref, ct_ref)
 
 
-def zonal_kernel(sz, shift_count, place, length, zt, zct, w_ref, owner, own, behind, ahead, *refs):
+def zonal_kernel(sz, shift_count, length, zt, zct, w_ref, owner, own, behind, ahead, *refs):
     others = refs[:shift_count]
-    out_ref, near_ref, b_ref, ca_ref, cb_ref, ct_ref = refs[shift_count:]
-    lon = place[0]
+    out_ref, below_ref, mid_ref, above_ref, b_ref, ca_ref, cb_ref, ct_ref = refs[shift_count:]
+    lon = lax.axis_index("lon")
     out_ref[...] = zt[...]
     ct_ref[...] = zct[...]
     ends = own[...] + behind[0 : 2 * sz.packet, :] + ahead[0 : 2 * sz.packet, :]
@@ -229,7 +230,7 @@
                     ref[pl.ds(row, 1), :] = head[at : at + 1]
     substeps(sz, w_ref, out_ref, b_ref, ca_ref, cb_ref, ct_ref)
     scale = GLON_DEV / (3.0 * CELLS_DEV)
-    near = near_ref.shape[0] // sz.rows
+    near = 8
     for r in range(sz.rows):
         column = lon * GLON_DEV - 1 + lax.broadcasted_iota(jnp.int32, (near, sz.cells), 0)
         cell = lon * sz.cells + lax.broadcasted_iota(jnp.int32, (near, sz.cells), 1)
@@ -245,14 +246,18 @@
                 change = part if change is None else change + part
             halves.append(change)
         change = jnp.concatenate(halves, axis=0) * scale
-        near_ref[pl.ds(r, near, stride=sz.rows), :] = jnp.dot(
+        sums = jnp.dot(
             table.astype(jnp.float32), change, precision=lax.Precision.HIGHEST,
             preferred_element_type=jnp.float32,
         )
-
-
-def turn_out(sz, place, length, mt, zt, z_ref, m_out, z_out):
-    lon = place[0]
+        below_ref[r : r + 1, :] = sums[0:1]
+        above_ref[r : r + 1, :] = sums[GLON_DEV + 1 : GLON_DEV + 2]
+        for g in range(GLON_DEV):
+            mid_ref[g * sz.rows + r : g * sz.rows + r + 1, :] = sums[g + 1 : g + 2]
+
+
+def turn_out(sz, length, mt, zt, z_ref, m_out, z_out):
+    lon = lax.axis_index("lon")
     cell = lon * sz.cells + lax.broadcasted_iota(jnp.int32, (sz.lanes, sz.cells), 1)
     for zonal, src, dst in ((False, mt, m_out), (True, zt, z_out)):
         for w in range(sz.wid):
@@ -269,7 +274,14 @@
                 dst[at, :] = value
 
 
-def call(body, outs, smem, vmem, scratch=(), name=None):
+def finish(sz, mid, from_left, from_right, out_ref):
+    end = (GLON_DEV - 1) * sz.rows
+    out_ref[0 : sz.rows, :] = mid[0 : sz.rows, :] + from_left[...]
+    out_ref[sz.rows : end, :] = mid[sz.rows : end, :]
+    out_ref[end:, :] = mid[end:, :] + from_right[...]
+
+
+def call(body, outs, smem, vmem, scratch=(), name=None, flops=1 << 20):
     return pl.pallas_call(
         body,
         out_shape=outs,
@@ -277,6 +289,8 @@
         + [pl.BlockSpec(memory_space=pltpu.VMEM)] * vmem,
         out_specs=[pl.BlockSpec(memory_space=pltpu.VMEM)] * len(outs),
         scratch_shapes=list(scratch),
+        compiler_params=pltpu.CompilerParams(vmem_limit_bytes=VMEM_GRANT),
+        cost_estimate=pl.CostEstimate(flops=flops, bytes_accessed=4 << 20, transcendentals=0),
         name=name,
     )
 
@@ -294,9 +308,6 @@
     lon_count = lax.axis_size("lon")
     lat_count = lax.axis_size("lat")
     lat_two = lat_count == 2
-    place = jnp.stack(
-        [lax.axis_index("lon"), lax.axis_index("lat"), jnp.int32(lat_count - 1)]
-    ).astype(jnp.int32)
     flat = lambda a: a.reshape(-1, sz.cells)
     z, m = flat(zonal_state), flat(merid_state)
     state_rows = sz.wid * sz.span * sz.group
@@ -304,7 +315,7 @@
     packet = sz.packet
     lanes = sz.lanes
     zt, zct, mt, mct, weights, zfirst, zlast, ht, htp, mlow, mhigh = call(
-        functools.partial(turn_in, sz, lat_two),
+        functools.partial(turn_in, sz, lat_two, lat_count),
         (
             f32(state_rows, lanes), f32(courant_rows, lanes),
             f32(state_rows, lanes), f32(courant_rows, lanes),
@@ -312,14 +323,14 @@
             f32(packet, lanes), f32(packet, lanes), f32(2 * packet, lanes),
             f32(3 * packet, lanes), f32(packet, lanes), f32(packet, lanes),
         ),
-        2, 5,
+        1, 5,
         (
             pltpu.VMEM((sz.cells + 16, lanes), jnp.float32),
             pltpu.VMEM((packet, lanes), jnp.float32),
             pltpu.VMEM((packet, lanes), jnp.float32),
         ),
         "turn_in",
-    )(place, zonal_length, z, flat(zonal_courant), m, flat(merid_courant),
+    )(zonal_length, z, flat(zonal_courant), m, flat(merid_courant),
       mixing.reshape(lanes, sz.lev))
     pole = shifted(htp, "lon", lon_count // 2)
     if lat_two:
@@ -356,25 +367,28 @@
         pltpu.VMEM((courant_rows, lanes), jnp.float32),
     )
     (mt_next,) = call(
-        functools.partial(merid_kernel, sz, lat_two),
-        (f32(state_rows, lanes),), 1, 7, work, "merid",
-    )(place, mt, mct, weights, pole, lat_a, lat_b, mhigh)
-    near = 8
-    zt_next, near_terms = call(
+        functools.partial(merid_kernel, sz, lat_two, lat_count),
+        (f32(state_rows, lanes),), 0, 7, work, "merid", 1 << 32,
+    )(mt, mct, weights, pole, lat_a, lat_b, mhigh)
+    own, mt_next = lax.optimization_barrier((own, mt_next))
+    zt_next, below, mid, above = call(
         functools.partial(zonal_kernel, sz, len(others)),
-        (f32(state_rows, lanes), f32(near * sz.rows, lanes)), 2, 7 + len(others), work, "zonal",
-    )(place, zonal_length, zt, zct, weights, zonal_owner, own, behind, ahead, *others)
-    near_terms = near_terms.reshape(near, sz.rows, lanes)
-    from_right = shifted(near_terms[0], "lon", -1)
-    from_left = shifted(near_terms[GLON_DEV + 1], "lon", 1)
+        (
+            f32(state_rows, lanes), f32(sz.rows, lanes), f32(GLON_DEV * sz.rows, lanes),
+            f32(sz.rows, lanes),
+        ),
+        1, 7 + len(others), work, "zonal", 1 << 32,
+    )(zonal_length, zt, zct, weights, zonal_owner, own, behind, ahead, *others)
+    from_right = shifted(below, "lon", -1)
+    from_left = shifted(above, "lon", 1)
     m_next, z_next = call(
         functools.partial(turn_out, sz),
-        (f32(*m.shape), f32(*z.shape)), 2, 3, (), "turn_out",
-    )(place, zonal_length, mt_next, zt_next, z)
-    coupling = near_terms[1 : GLON_DEV + 1]
-    coupling = jnp.concatenate(
-        [coupling[:1] + from_left[None], coupling[1:-1], coupling[-1:] + from_right[None]]
-    )
+        (f32(*m.shape), f32(*z.shape)), 1, 3, (), "turn_out", 1 << 32,
+    )(zonal_length, mt_next, zt_next, z)
+    (coupling,) = call(
+        functools.partial(finish, sz), (f32(*mid.shape),), 0, 3, (), "finish",
+    )(mid, from_left, from_right)
+    coupling = coupling.reshape(GLON_DEV, sz.rows, lanes)
     return z_next.reshape(zonal_state.shape), m_next.reshape(merid_state.shape), coupling
 
 

time: 53.3 us -> 40.8 us (0.77)
  waiting for transfers between devices: 14.9 us -> 6.6 us
  Pallas kernels: 17.3 us -> 9.32 us
  starting transfers between devices: 14.1 us -> 18.4 us
  other arithmetic: 2.66 us -> 0 us
  local copies, waits for them, and re-layouts: 3.34 us -> 5.44 us
    ppermute x9, waiting for transfers between devices: 14.9 us -> 6.6 us  [shifted(): lax.ppermute(value, axis, [(i, (i + steps) % count) for i in range(count)])]
    pallas_call x3 -> x4, Pallas kernels: 11.2 us -> 6.24 us  [the longest x1 2.21 us: shards(): call(functools.partial(merid_kernel, sz, lat_two, lat_count), (f32(state_...]
    ppermute x9, starting transfers between devices: 14.1 us -> 18.4 us  [shifted(): lax.ppermute(value, axis, [(i, (i + steps) % count) for i in range(count)])]
    unnamed x16, local copies, waits for them, and re-layouts: 1.98 us -> 5.44 us
    pallas_call x1, Pallas kernels: 1.72 us -> 0.02 us  [shards(): call(functools.partial(combine, len(parts), packet), (f32(2 * packet, lan...]
    add x2 -> x0, other arithmetic: 1.44 us -> none  [the longest x1 0.75 us: shards(): coupling[:1] + from_left[None]]
    slice x2 -> x0, local copies, waits for them, and re-layouts: 1.36 us -> none  [the longest x1 0.69 us: shards(): from_left = shifted(near_terms[GLON_DEV + 1], 'lon', 1)]
    pallas_call x1, Pallas kernels: 4.41 us -> 3.06 us  [shards(): call(functools.partial(zonal_kernel, sz, len(others)), (f32(state_rows, l...]
  transfers between devices with their start and end apart: 9 -> 9, of which waited for: 4 -> 3; matrix products, arithmetic and copies ran while one was open for 3% -> 0% of each run, Pallas kernels for 14% -> 10%
where the time goes in v2:
time: 40.8 us; the launch traced here: 40.5 us
  starting transfers between devices  18.4 us (45%)
  Pallas kernels  9.32 us (23%)
  waiting for transfers between devices  6.6 us (16%)
  local copies, waits for them, and re-layouts  5.44 us (13%)
  between operations  0.7 us (2%)
    ppermute x9, starting transfers between devices, shifted(): lax.ppermute(value, axis, [(i, (i + steps) % count) for i in range(count)])  18.4 us
    ppermute x9, waiting for transfers between devices, shifted(): lax.ppermute(value, axis, [(i, (i + steps) % count) for i in range(count)])  6.6 us
    unnamed x16, local copies, waits for them, and re-layouts  5.44 us
    pallas_call x1, Pallas kernels, shards(): call(functools.partial(zonal_kernel, sz, len(others)), (f32(state_rows, l...  3.06 us
    pallas_call x1, Pallas kernels, shards(): call(functools.partial(merid_kernel, sz, lat_two, lat_count), (f32(state_...  2.21 us
    pallas_call x1, Pallas kernels, shards(): call(functools.partial(turn_out, sz), (f32(*m.shape), f32(*z.shape)), 1,...  1.95 us
    pallas_call x1, Pallas kernels, shards(): call(functools.partial(turn_in, sz, lat_two, lat_count), (f32(state_rows,...  1.47 us
  transfers between devices with their start and end apart: 9, of which 3 were waited for; matrix products, arithmetic and copies ran while one was open for 0% of the time, Pallas kernels for 10%

profile of v2, /device:TPU:0, one launch (start us, length us, event | category | flops | bytes accessed | tf_op | source)
XLA Modules:
  0.0 40.5 jit_solution(2624722117886425408)
XLA Ops:
  0.6 0.6 %copy-done.6 = s32[4]{0:T(128)S(1)} copy-done((s32[4]{0:T(128)S(1)}, s32[4]{0:T(128)}, u32[]{:S(2)}) %copy-start.6) | copy-done | bytes 40
  1.3 1.1 %copy-done = f32[4,32,3,4,128]{4,3,2,1,0:T(4,128)S(1)} copy-done((f32[4,32,3,4,128]{4,3,2,1,0:T(4,128)S(1)}, f32[4,32,3,4,128]{4,3,2,1,0:T(4,128)}, u32[]{:S(2)}) %copy-start) | copy-done | bytes 786456
  2.4 1.1 %copy-done.1 = f32[4,32,3,4,128]{4,3,2,1,0:T(4,128)S(1)} copy-done((f32[4,32,3,4,128]{4,3,2,1,0:T(4,128)S(1)}, f32[4,32,3,4,128]{4,3,2,1,0:T(4,128)}, u32[]{:S(2)}) %copy-start.1) | copy-done | bytes 786456
  3.6 0.8 %copy-done.3 = f32[32,4,128]{2,1,0:T(4,128)S(1)} copy-done((f32[32,4,128]{2,1,0:T(4,128)S(1)}, f32[32,4,128]{2,1,0:T(4,128)}, u32[]{:S(2)}) %copy-start.3) | copy-done | bytes 65560
  4.4 0.8 %copy-done.4 = f32[32,4,128]{2,1,0:T(4,128)S(1)} copy-done((f32[32,4,128]{2,1,0:T(4,128)S(1)}, f32[32,4,128]{2,1,0:T(4,128)}, u32[]{:S(2)}) %copy-start.4) | copy-done | bytes 65560
  5.2 0.8 %copy-done.5 = f32[4,32,32]{2,1,0:T(8,128)S(1)} copy-done((f32[4,32,32]{2,1,0:T(8,128)S(1)}, f32[4,32,32]{2,1,0:T(8,128)}, u32[]{:S(2)}) %copy-start.5) | copy-done | bytes 16408
  6.1 1.5 %turn_in.1 = (f32[1920,128]{1,0:T(8,128)S(1)}, f32[640,128]{1,0:T(8,128)S(1)}, f32[1920,128]{1,0:T(8,128)S(1)}, f32[640,128]{1,0:T(8,128)S(1)}, bf16[256,256]{1,...) custom-call(s32[4]{0:T(128)S(1)} %copy-done.6, ...), custom_call_target="tpu_custom_call" | custom-call | flops 1048576 | bytes 4194304 | tf_op jit(solution)/shard_map/turn_in/pallas_call | solution.py:317
  7.6 4.1 %collective-permute-start.1 = (f32[192,128]{1,0:T(8,128)S(1)}, f32[192,128]{1,0:T(8,128)S(1)}, u32[]{:S(2)}, u32[]{:S(2)}) collective-permute-start(f32[192,128]{1,0:T(8,128)S(1)} %get-tuple-element.28), channel_id=1, source_target_pairs={{0,16},{2,18},{4,20},{6,22},{8,24},{10,26},{12,28},{14,30},{16,0},... | collective-permute-start | bytes 294920 | tf_op jit(solution)/shard_map/ppermute | solution.py:300
  11.7 1.6 %collective-permute-start = (f32[128,128]{1,0:T(8,128)S(1)}, f32[128,128]{1,0:T(8,128)S(1)}, u32[]{:S(2)}, u32[]{:S(2)}) collective-permute-start(f32[128,128]{1,0:T(8,128)S(1)} %get-tuple-element.25.refs_0_), channel_id=1, source_target_pairs={{0,8},{2,10},{4,12},{6,14},{8,16},{10,18},{12,20},{14,22},{16,24},... | collective-permute-start | bytes 196616 | tf_op jit(solution)/shard_map/ppermute | solution.py:300
  13.3 2.2 %collective-permute-start.2 = (f32[128,128]{1,0:T(8,128)S(1)}, f32[128,128]{1,0:T(8,128)S(1)}, u32[]{:S(2)}, u32[]{:S(2)}) collective-permute-start(f32[128,128]{1,0:T(8,128)S(1)} %get-tuple-element.25.refs_0_), channel_id=1, source_target_pairs={{0,24},{2,26},{4,28},{6,30},{8,0},{10,2},{12,4},{14,6},{16,8},{18,... | collective-permute-start | bytes 196616 | tf_op jit(solution)/shard_map/ppermute | solution.py:300
  15.5 1.5 %collective-permute-start.3 = (f32[64,128]{1,0:T(8,128)S(1)}, f32[64,128]{1,0:T(8,128)S(1)}, u32[]{:S(2)}, u32[]{:S(2)}) collective-permute-start(f32[64,128]{1,0:T(8,128)S(1)} %get-tuple-element.33), channel_id=1, source_target_pairs={{0,1},{1,0},{2,3},{3,2},{4,5},{5,4},{6,7},{7,6},{8,9},{9,8},{10,11... | collective-permute-start | bytes 98312 | tf_op jit(solution)/shard_map/ppermute | solution.py:300
  17.0 0.8 %collective-permute-done.refs_3_ = f32[128,128]{1,0:T(8,128)S(1)} collective-permute-done((f32[128,128]{1,0:T(8,128)S(1)}, f32[128,128]{1,0:T(8,128)S(1)}, u32[]{:S(2)}, u32[]{:S(2)}) %collective-permute-start) | collective-permute-done | bytes 65568 | tf_op jit(solution)/shard_map/ppermute | solution.py:300
  17.9 1.0 %collective-permute-done.2.refs_5_ = f32[128,128]{1,0:T(8,128)S(1)} collective-permute-done((f32[128,128]{1,0:T(8,128)S(1)}, f32[128,128]{1,0:T(8,128)S(1)}, u32[]{:S(2)}, u32[]{:S(2)}) %collective-permute-start.2) | collective-permute-done | bytes 65568 | tf_op jit(solution)/shard_map/ppermute | solution.py:300
  18.9 0.0 collective-permute-done.1.refs_4_.pole
  18.9 0.1 collective-permute-start.4
  19.0 4.4 %collective-permute-start.5 = (f32[192,128]{1,0:T(8,128)S(1)}, f32[192,128]{1,0:T(8,128)S(1)}, u32[]{:S(2)}, u32[]{:S(2)}) collective-permute-start(f32[192,128]{1,0:T(8,128)S(1)} %get-tuple-element.40), channel_id=1, source_target_pairs={{0,30},{2,0},{4,2},{6,4},{8,6},{10,8},{12,10},{14,12},{16,14},{18,... | collective-permute-start | bytes 294920 | tf_op jit(solution)/shard_map/ppermute | solution.py:300
  23.4 0.0 collective-permute-start.6
  23.4 0.0 collective-permute-done.3.lat_a.lat_b
  23.4 2.2 %merid.1.mt = f32[1920,128]{1,0:T(8,128)S(1)} custom-call(f32[1920,128]{1,0:T(8,128)S(1)} %get-tuple-element.30.mt, f32[640,128]{1,0:T(8,128)S(1)} %get-tuple-element.31.mct, bf16[256,256]{1,0:T(8,128)(2,1)S(1)} %get-tuple-element.32.w_ref, f32[192,128]{1,0:T(8,128)S(1)} %collective-permute-done.1.refs_4_.pole, ...), custom_call_target="tpu_custom_call" | custom-call | flops 4294967296 | bytes 4194304 | tf_op jit(solution)/shard_map/merid/pallas_call | solution.py:369
  25.6 0.0 copy-start.7
  25.7 4.7 %collective-permute-done.6.refs_0_ = f32[128,128]{1,0:T(8,128)S(1)} collective-permute-done((f32[128,128]{1,0:T(8,128)S(1)}, f32[128,128]{1,0:T(8,128)S(1)}, u32[]{:S(2)}, u32[]{:S(2)}) %collective-permute-start.6) | collective-permute-done | bytes 65568 | tf_op jit(solution)/shard_map/ppermute | solution.py:300
  30.4 0.0 collective-permute-done.4.behind
  30.4 0.0 collective-permute-done.5.ahead
  30.4 0.0 copy-start.2
  30.4 3.1 %zonal.1 = (f32[1920,128]{1,0:T(8,128)S(1)}, f32[4,128]{1,0:T(4,128)S(1)}, f32[16,128]{1,0:T(8,128)S(1)}, f32[4,128]{1,0:T(4,128)S(1)}) custom-call(s32[4]{0:T(128)S(1)} %copy-done.6, f32[1920,128]{1,0:T(8,128)S(1)} %get-tuple-element.36.zt, f32[640,128]{1,0:T(8,128)S(1)} %get-tuple-element.37.zct, bf16[256,256]{1,0:T(8,128)(2,1)S(1)} %get-tuple-element.32.w_ref, ...), custom_call_target="tpu_custom_call" | custom-call | flops 4294967296 | bytes 4194304 | tf_op jit(solution)/shard_map/zonal/pallas_call | solution.py:374
  33.5 0.0 collective-permute-start.7
  33.5 4.5 %collective-permute-start.8 = (f32[4,128]{1,0:T(4,128)S(1)}, f32[4,128]{1,0:T(4,128)S(1)}, u32[]{:S(2)}, u32[]{:S(2)}) collective-permute-start(f32[4,128]{1,0:T(4,128)S(1)} %get-tuple-element.46), channel_id=1, source_target_pairs={{0,30},{2,0},{4,2},{6,4},{8,6},{10,8},{12,10},{14,12},{16,14},{18,... | collective-permute-start | bytes 6152 | tf_op jit(solution)/shard_map/ppermute | solution.py:300
  37.9 0.0 copy-done.2
  37.9 1.9 %turn_out.1 = (f32[1536,128]{1,0:T(8,128)}, f32[1536,128]{1,0:T(8,128)}) custom-call(s32[4]{0:T(128)S(1)} %copy-done.6, f32[1920,128]{1,0:T(8,128)S(1)} %merid.1.mt, f32[1920,128]{1,0:T(8,128)S(1)} %get-tuple-element.41.zt, f32[1536,128]{1,0:T(8,128)S(1)} %bitcast.10), custom_call_target="tpu_custom_call" | custom-call | flops 4294967296 | bytes 4194304 | tf_op jit(solution)/shard_map/turn_out/pallas_call | solution.py:384
  39.9 0.0 collective-permute-done.7.from_left
  39.9 0.0 collective-permute-done.8.from_right
  39.9 0.6 %finish.1 = f32[16,128]{1,0:T(8,128)} custom-call(f32[16,128]{1,0:T(8,128)S(1)} %get-tuple-element.44.mid, f32[4,128]{1,0:T(4,128)S(1)} %collective-permute-done.7.from_left, f32[4,128]{1,0:T(4,128)S(1)} %collective-permute-done.8.from_right), custom_call_target="tpu_custom_call" | custom-call | flops 1048576 | bytes 4194304 | tf_op jit(solution)/shard_map/finish/pallas_call | solution.py:388
  (8 shorter events, 0.0 us)
Async XLA Ops:
  0.6 0.7 %copy-start.6 = (s32[4]{0:T(128)S(1)}, s32[4]{0:T(128)}, u32[]{:S(2)}) copy-start(s32[4]{0:T(128)} %length.5) | copy-start | bytes 52
  1.3 1.1 %copy-start = (f32[4,32,3,4,128]{4,3,2,1,0:T(4,128)S(1)}, f32[4,32,3,4,128]{4,3,2,1,0:T(4,128)}, u32[]{:S(2)}) copy-start(f32[4,32,3,4,128]{4,3,2,1,0:T(4,128)} %param.11) | copy-start | bytes 2359300
  2.4 1.1 %copy-start.1 = (f32[4,32,3,4,128]{4,3,2,1,0:T(4,128)S(1)}, f32[4,32,3,4,128]{4,3,2,1,0:T(4,128)}, u32[]{:S(2)}) copy-start(f32[4,32,3,4,128]{4,3,2,1,0:T(4,128)} %param.7) | copy-start | bytes 2359300
  3.6 0.8 %copy-start.3 = (f32[32,4,128]{2,1,0:T(4,128)S(1)}, f32[32,4,128]{2,1,0:T(4,128)}, u32[]{:S(2)}) copy-start(f32[32,4,128]{2,1,0:T(4,128)} %param.8) | copy-start | bytes 196612
  4.4 0.8 %copy-start.4 = (f32[32,4,128]{2,1,0:T(4,128)S(1)}, f32[32,4,128]{2,1,0:T(4,128)}, u32[]{:S(2)}) copy-start(f32[32,4,128]{2,1,0:T(4,128)} %param.12) | copy-start | bytes 196612
  5.2 0.8 %copy-start.5 = (f32[4,32,32]{2,1,0:T(8,128)S(1)}, f32[4,32,32]{2,1,0:T(8,128)}, u32[]{:S(2)}) copy-start(f32[4,32,32]{2,1,0:T(8,128)} %param.13) | copy-start | bytes 49156
  7.6 11.3 %collective-permute-start.1 = (f32[192,128]{1,0:T(8,128)S(1)}, f32[192,128]{1,0:T(8,128)S(1)}, u32[]{:S(2)}, u32[]{:S(2)}) collective-permute-start(f32[192,128]{1,0:T(8,128)S(1)} %get-tuple-element.28), channel_id=1, source_target_pairs={{0,16},{2,18},{4,20},{6,22},{8,24},{10,26},{12,28},{14,30},{16,0},... | collective-permute-start | bytes 294920 | tf_op jit(solution)/shard_map/ppermute | solution.py:300
  11.7 6.2 %collective-permute-start = (f32[128,128]{1,0:T(8,128)S(1)}, f32[128,128]{1,0:T(8,128)S(1)}, u32[]{:S(2)}, u32[]{:S(2)}) collective-permute-start(f32[128,128]{1,0:T(8,128)S(1)} %get-tuple-element.25.refs_0_), channel_id=1, source_target_pairs={{0,8},{2,10},{4,12},{6,14},{8,16},{10,18},{12,20},{14,22},{16,24},... | collective-permute-start | bytes 196616 | tf_op jit(solution)/shard_map/ppermute | solution.py:300
  13.3 5.6 %collective-permute-start.2 = (f32[128,128]{1,0:T(8,128)S(1)}, f32[128,128]{1,0:T(8,128)S(1)}, u32[]{:S(2)}, u32[]{:S(2)}) collective-permute-start(f32[128,128]{1,0:T(8,128)S(1)} %get-tuple-element.25.refs_0_), channel_id=1, source_target_pairs={{0,24},{2,26},{4,28},{6,30},{8,0},{10,2},{12,4},{14,6},{16,8},{18,... | collective-permute-start | bytes 196616 | tf_op jit(solution)/shard_map/ppermute | solution.py:300
  15.5 7.9 %collective-permute-start.3 = (f32[64,128]{1,0:T(8,128)S(1)}, f32[64,128]{1,0:T(8,128)S(1)}, u32[]{:S(2)}, u32[]{:S(2)}) collective-permute-start(f32[64,128]{1,0:T(8,128)S(1)} %get-tuple-element.33), channel_id=1, source_target_pairs={{0,1},{1,0},{2,3},{3,2},{4,5},{5,4},{6,7},{7,6},{8,9},{9,8},{10,11... | collective-permute-start | bytes 98312 | tf_op jit(solution)/shard_map/ppermute | solution.py:300
  18.9 11.5 %collective-permute-start.4 = (f32[192,128]{1,0:T(8,128)S(1)}, f32[192,128]{1,0:T(8,128)S(1)}, u32[]{:S(2)}, u32[]{:S(2)}) collective-permute-start(f32[192,128]{1,0:T(8,128)S(1)} %get-tuple-element.39), channel_id=1, source_target_pairs={{0,2},{2,4},{4,6},{6,8},{8,10},{10,12},{12,14},{14,16},{16,18},{18... | collective-permute-start | bytes 294920 | tf_op jit(solution)/shard_map/ppermute | solution.py:300
  19.0 11.4 %collective-permute-start.5 = (f32[192,128]{1,0:T(8,128)S(1)}, f32[192,128]{1,0:T(8,128)S(1)}, u32[]{:S(2)}, u32[]{:S(2)}) collective-permute-start(f32[192,128]{1,0:T(8,128)S(1)} %get-tuple-element.40), channel_id=1, source_target_pairs={{0,30},{2,0},{4,2},{6,4},{8,6},{10,8},{12,10},{14,12},{16,14},{18,... | collective-permute-start | bytes 294920 | tf_op jit(solution)/shard_map/ppermute | solution.py:300
  23.4 7.0 %collective-permute-start.6 = (f32[128,128]{1,0:T(8,128)S(1)}, f32[128,128]{1,0:T(8,128)S(1)}, u32[]{:S(2)}, u32[]{:S(2)}) collective-permute-start(f32[128,128]{1,0:T(8,128)S(1)} %get-tuple-element.38.own), channel_id=1, source_target_pairs={{0,4},{2,6},{4,8},{6,10},{8,12},{10,14},{12,16},{14,18},{16,20},{1... | collective-permute-start | bytes 196616 | tf_op jit(solution)/shard_map/ppermute | solution.py:300
  25.6 4.7 %copy-start.7 = (s32[4,128]{1,0:T(4,128)S(1)}, s32[4,128]{1,0:T(4,128)}, u32[]{:S(2)}) copy-start(s32[4,128]{1,0:T(4,128)} %owner.1) | copy-start | bytes 6148
  30.4 7.5 %copy-start.2 = (f32[4,32,3,4,128]{4,3,2,1,0:T(4,128)S(1)}, f32[4,32,3,4,128]{4,3,2,1,0:T(4,128)}, u32[]{:S(2)}) copy-start(f32[4,32,3,4,128]{4,3,2,1,0:T(4,128)} %param.7) | copy-start | bytes 2359300
  33.5 6.4 %collective-permute-start.7 = (f32[4,128]{1,0:T(4,128)S(1)}, f32[4,128]{1,0:T(4,128)S(1)}, u32[]{:S(2)}, u32[]{:S(2)}) collective-permute-start(f32[4,128]{1,0:T(4,128)S(1)} %get-tuple-element.45), channel_id=1, source_target_pairs={{0,2},{2,4},{4,6},{6,8},{8,10},{10,12},{12,14},{14,16},{16,18},{18... | collective-permute-start | bytes 6152 | tf_op jit(solution)/shard_map/ppermute | solution.py:300
  33.5 6.4 %collective-permute-start.8 = (f32[4,128]{1,0:T(4,128)S(1)}, f32[4,128]{1,0:T(4,128)S(1)}, u32[]{:S(2)}, u32[]{:S(2)}) collective-permute-start(f32[4,128]{1,0:T(4,128)S(1)} %get-tuple-element.46), channel_id=1, source_target_pairs={{0,30},{2,0},{4,2},{6,4},{8,6},{10,8},{12,10},{14,12},{16,14},{18,... | collective-permute-start | bytes 6152 | tf_op jit(solution)/shard_map/ppermute | solution.py:300

commit v3 on v2

--- a/solution.py
+++ b/solution.py
@@ -44,9 +44,18 @@
     ]
 
 
-def turn_in(sz, lat_two, lat_count, length, z_ref, zc_ref, m_ref, mc_ref, mix_ref,
+def turn_in(sz, lat_two, lat_count, length_ref, z_ref, zc_ref, m_ref, mc_ref, mix_ref,
             zt_ref, zct_ref, mt_ref, mct_ref, w_ref, zfirst, zlast, ht, htp, mlow, mhigh,
-            tile, low, high):
+            tile, low, high, z_in, zc_in, m_in, mc_in, mix_in, length, sems):
+    copies = [
+        pltpu.make_async_copy(source, target, sems.at[n])
+        for n, (source, target) in enumerate((
+            (length_ref, length), (m_ref, m_in), (mc_ref, mc_in), (z_ref, z_in),
+            (zc_ref, zc_in), (mix_ref, mix_in),
+        ))
+    ]
+    for copy in copies:
+        copy.start()
     lon = lax.axis_index("lon")
     lat = lax.axis_index("lat")
     last = lat_count - 1
@@ -73,8 +82,15 @@
             high[at, :] = finish
 
     for zonal, s_ref, c_ref, st_ref, ct_ref in (
-        (False, m_ref, mc_ref, mt_ref, mct_ref), (True, z_ref, zc_ref, zt_ref, zct_ref)
+        (False, m_in, mc_in, mt_ref, mct_ref), (True, z_in, zc_in, zt_ref, zct_ref)
     ):
+        if zonal:
+            copies[0].wait()
+            copies[3].wait()
+            copies[4].wait()
+        else:
+            copies[1].wait()
+            copies[2].wait()
         for r in range(sz.rows):
             for w in range(sz.wid):
                 slot = w * sz.rows + r
@@ -92,7 +108,8 @@
     else:
         mlow[...] = lows
         mhigh[...] = highs
-    turned = mix_ref[...].T
+    copies[5].wait()
+    turned = mix_in[...].T
     full = jnp.concatenate([turned] * sz.nv, axis=0)
     shape = (sz.lanes, sz.lanes)
     source = lax.broadcasted_iota(jnp.int32, shape, 0)
@@ -192,9 +209,17 @@
     substeps(sz, w_ref, out_ref, b_ref, ca_ref, cb_ref, ct_ref)
 
 
-def zonal_kernel(sz, shift_count, length, zt, zct, w_ref, owner, own, behind, ahead, *refs):
+def zonal_kernel(sz, shift_count, length_ref, owner_ref, zt, zct, w_ref, own, behind, ahead, *refs):
     others = refs[:shift_count]
-    out_ref, below_ref, mid_ref, above_ref, b_ref, ca_ref, cb_ref, ct_ref = refs[shift_count:]
+    out_ref, below_ref, mid_ref, above_ref, b_ref, ca_ref, cb_ref, ct_ref, length, owner, sems = (
+        refs[shift_count:]
+    )
+    copies = [
+        pltpu.make_async_copy(length_ref, length, sems.at[0]),
+        pltpu.make_async_copy(owner_ref, owner, sems.at[1]),
+    ]
+    for copy in copies:
+        copy.start()
     lon = lax.axis_index("lon")
     out_ref[...] = zt[...]
     ct_ref[...] = zct[...]
@@ -216,6 +241,7 @@
             ref[row : row + 1, :] = left[at : at + 1]
             row = (begin + PAD + SUB + sz.half + d) * sz.group + sz.rows + r
             ref[row : row + 1, :] = right[at : at + 1]
+    copies[0].wait()
     for r in range(sz.rows):
         past = length[r] - lon * sz.cells
         for h in range(2):
@@ -231,6 +257,7 @@
     substeps(sz, w_ref, out_ref, b_ref, ca_ref, cb_ref, ct_ref)
     scale = GLON_DEV / (3.0 * CELLS_DEV)
     near = 8
+    copies[1].wait()
     for r in range(sz.rows):
         column = lon * GLON_DEV - 1 + lax.broadcasted_iota(jnp.int32, (near, sz.cells), 0)
         cell = lon * sz.cells + lax.broadcasted_iota(jnp.int32, (near, sz.cells), 1)
@@ -256,10 +283,20 @@
             mid_ref[g * sz.rows + r : g * sz.rows + r + 1, :] = sums[g + 1 : g + 2]
 
 
-def turn_out(sz, length, mt, zt, z_ref, m_out, z_out):
+def turn_out(sz, length_ref, z_ref, mt, zt, m_out, z_out, m_own, z_own, z_in, length, sems):
+    reads = [
+        pltpu.make_async_copy(length_ref, length, sems.at[0]),
+        pltpu.make_async_copy(z_ref, z_in, sems.at[1]),
+    ]
+    for copy in reads:
+        copy.start()
+    writes = []
     lon = lax.axis_index("lon")
     cell = lon * sz.cells + lax.broadcasted_iota(jnp.int32, (sz.lanes, sz.cells), 1)
-    for zonal, src, dst in ((False, mt, m_out), (True, zt, z_out)):
+    for zonal, src, dst, out in ((False, mt, m_own, m_out), (True, zt, z_own, z_out)):
+        if zonal:
+            for copy in reads:
+                copy.wait()
         for w in range(sz.wid):
             for r in range(sz.rows):
                 halves = [
@@ -270,8 +307,12 @@
                 value = jnp.concatenate(halves, axis=0).T
                 at = pl.ds(w * sz.rows + r, sz.lanes, stride=sz.wr)
                 if zonal:
-                    value = jnp.where(cell < length[r], value, z_ref[at, :])
+                    value = jnp.where(cell < length[r], value, z_in[at, :])
                 dst[at, :] = value
+        writes.append(pltpu.make_async_copy(dst, out, sems.at[2 + zonal]))
+        writes[-1].start()
+    for copy in writes:
+        copy.wait()
 
 
 def finish(sz, mid, from_left, from_right, out_ref):
@@ -281,13 +322,12 @@
     out_ref[end:, :] = mid[end:, :] + from_right[...]
 
 
-def call(body, outs, smem, vmem, scratch=(), name=None, flops=1 << 20):
+def call(body, outs, spaces, scratch=(), name=None, flops=1 << 20, out_space=pltpu.VMEM):
     return pl.pallas_call(
         body,
         out_shape=outs,
-        in_specs=[pl.BlockSpec(memory_space=pltpu.SMEM)] * smem
-        + [pl.BlockSpec(memory_space=pltpu.VMEM)] * vmem,
-        out_specs=[pl.BlockSpec(memory_space=pltpu.VMEM)] * len(outs),
+        in_specs=[pl.BlockSpec(memory_space=space) for space in spaces],
+        out_specs=[pl.BlockSpec(memory_space=out_space)] * len(outs),
         scratch_shapes=list(scratch),
         compiler_params=pltpu.CompilerParams(vmem_limit_bytes=VMEM_GRANT),
         cost_estimate=pl.CostEstimate(flops=flops, bytes_accessed=4 << 20, transcendentals=0),
@@ -304,12 +344,14 @@
     zonal_state, zonal_courant, zonal_length, zonal_owner, merid_state, merid_courant, mixing
 ):
     sz = Sizes(zonal_state.shape)
+    zonal_length = pltpu.with_memory_space_constraint(zonal_length, pltpu.HBM)
     f32 = lambda *shape: jax.ShapeDtypeStruct(shape, jnp.float32)
     lon_count = lax.axis_size("lon")
     lat_count = lax.axis_size("lat")
     lat_two = lat_count == 2
     flat = lambda a: a.reshape(-1, sz.cells)
-    z, m = flat(zonal_state), flat(merid_state)
+    hbm = lambda a: pltpu.with_memory_space_constraint(a, pltpu.HBM)
+    z, m = hbm(flat(zonal_state)), hbm(flat(merid_state))
     state_rows = sz.wid * sz.span * sz.group
     courant_rows = sz.span * sz.group
     packet = sz.packet
@@ -323,15 +365,22 @@
             f32(packet, lanes), f32(packet, lanes), f32(2 * packet, lanes),
             f32(3 * packet, lanes), f32(packet, lanes), f32(packet, lanes),
         ),
-        1, 5,
+        [pltpu.HBM] * 6,
         (
             pltpu.VMEM((sz.cells + 16, lanes), jnp.float32),
             pltpu.VMEM((packet, lanes), jnp.float32),
             pltpu.VMEM((packet, lanes), jnp.float32),
+            pltpu.VMEM(z.shape, jnp.float32),
+            pltpu.VMEM((sz.lev * sz.rows, sz.cells), jnp.float32),
+            pltpu.VMEM(m.shape, jnp.float32),
+            pltpu.VMEM((sz.lev * sz.rows, sz.cells), jnp.float32),
+            pltpu.VMEM((lanes, sz.lev), jnp.float32),
+            pltpu.SMEM((sz.rows,), jnp.int32),
+            pltpu.SemaphoreType.DMA((6,)),
         ),
         "turn_in",
-    )(zonal_length, z, flat(zonal_courant), m, flat(merid_courant),
-      mixing.reshape(lanes, sz.lev))
+    )(zonal_length, z, hbm(flat(zonal_courant)), m, hbm(flat(merid_courant)),
+      hbm(mixing.reshape(lanes, sz.lev)))
     pole = shifted(htp, "lon", lon_count // 2)
     if lat_two:
         lat_a = lat_b = shifted(mlow, "lat", 1)
@@ -355,7 +404,7 @@
         own, to_left, to_right = call(
             functools.partial(combine, len(parts), packet),
             (f32(2 * packet, lanes), f32(3 * packet, lanes), f32(3 * packet, lanes)),
-            0, 3 + len(parts), (), "combine",
+            [pltpu.VMEM] * (3 + len(parts)), (), "combine",
         )(own, zfirst, zlast, *parts)
     behind = shifted(to_right, "lon", 1)
     ahead = shifted(to_left, "lon", -1)
@@ -368,7 +417,7 @@
     )
     (mt_next,) = call(
         functools.partial(merid_kernel, sz, lat_two, lat_count),
-        (f32(state_rows, lanes),), 0, 7, work, "merid", 1 << 32,
+        (f32(state_rows, lanes),), [pltpu.VMEM] * 7, work, "merid", 1 << 32,
     )(mt, mct, weights, pole, lat_a, lat_b, mhigh)
     own, mt_next = lax.optimization_barrier((own, mt_next))
     zt_next, below, mid, above = call(
@@ -377,16 +426,28 @@
             f32(state_rows, lanes), f32(sz.rows, lanes), f32(GLON_DEV * sz.rows, lanes),
             f32(sz.rows, lanes),
         ),
-        1, 7 + len(others), work, "zonal", 1 << 32,
-    )(zonal_length, zt, zct, weights, zonal_owner, own, behind, ahead, *others)
+        [pltpu.HBM] * 2 + [pltpu.VMEM] * (6 + len(others)),
+        work + (
+            pltpu.SMEM((sz.rows,), jnp.int32),
+            pltpu.VMEM((sz.rows, sz.cells), jnp.int32),
+            pltpu.SemaphoreType.DMA((2,)),
+        ),
+        "zonal", 1 << 32,
+    )(zonal_length, zonal_owner, zt, zct, weights, own, behind, ahead, *others)
     from_right = shifted(below, "lon", -1)
     from_left = shifted(above, "lon", 1)
     m_next, z_next = call(
         functools.partial(turn_out, sz),
-        (f32(*m.shape), f32(*z.shape)), 1, 3, (), "turn_out", 1 << 32,
-    )(zonal_length, mt_next, zt_next, z)
+        (f32(*m.shape), f32(*z.shape)), [pltpu.HBM] * 2 + [pltpu.VMEM] * 2,
+        (
+            pltpu.VMEM(m.shape, jnp.float32), pltpu.VMEM(z.shape, jnp.float32),
+            pltpu.VMEM(z.shape, jnp.float32), pltpu.SMEM((sz.rows,), jnp.int32),
+            pltpu.SemaphoreType.DMA((4,)),
+        ),
+        "turn_out", 1 << 32, pltpu.HBM,
+    )(zonal_length, z, mt_next, zt_next)
     (coupling,) = call(
-        functools.partial(finish, sz), (f32(*mid.shape),), 0, 3, (), "finish",
+        functools.partial(finish, sz), (f32(*mid.shape),), [pltpu.VMEM] * 3, (), "finish",
     )(mid, from_left, from_right)
     coupling = coupling.reshape(GLON_DEV, sz.rows, lanes)
     return z_next.reshape(zonal_state.shape), m_next.reshape(merid_state.shape), coupling

time: 40.8 us -> 36.9 us (0.904)
  local copies, waits for them, and re-layouts: 5.44 us -> 0.01 us
  Pallas kernels: 9.32 us -> 10.6 us
    unnamed x16 -> x2, local copies, waits for them, and re-layouts: 5.44 us -> 0.01 us
    pallas_call x1, Pallas kernels: 1.47 us -> 2.31 us  [shards(): call(functools.partial(turn_in, sz, lat_two, lat_count), (f32(state_rows,...]
    pallas_call x2, Pallas kernels: 2.55 us -> 3.38 us  [the longest x1 2.78 us: shards(): call(functools.partial(turn_out, sz), (f32(*m.shape), f32(*z.shape)), [pl...]
  transfers between devices with their start and end apart: 9 -> 9, of which waited for: 3 -> 3; matrix products, arithmetic and copies ran while one was open for 0% -> 0% of each run, Pallas kernels for 10% -> 13%
where the time goes in v3:
time: 36.9 us; the launch traced here: 36.7 us
  starting transfers between devices  18.5 us (50%)
  Pallas kernels  10.6 us (29%)
  waiting for transfers between devices  6.91 us (19%)
  between operations  0.72 us (2%)
    ppermute x9, starting transfers between devices, shifted(): lax.ppermute(value, axis, [(i, (i + steps) % count) for i in range(count)])  18.5 us
    ppermute x9, waiting for transfers between devices, shifted(): lax.ppermute(value, axis, [(i, (i + steps) % count) for i in range(count)])  6.91 us
    pallas_call x1, Pallas kernels, shards(): call(functools.partial(zonal_kernel, sz, len(others)), (f32(state_rows, l...  3.03 us
    pallas_call x1, Pallas kernels, shards(): call(functools.partial(turn_out, sz), (f32(*m.shape), f32(*z.shape)), [pl...  2.78 us
    pallas_call x1, Pallas kernels, shards(): call(functools.partial(turn_in, sz, lat_two, lat_count), (f32(state_rows,...  2.31 us
    pallas_call x1, Pallas kernels, shards(): call(functools.partial(merid_kernel, sz, lat_two, lat_count), (f32(state_...  1.9 us
  transfers between devices with their start and end apart: 9, of which 3 were waited for; matrix products, arithmetic and copies ran while one was open for 0% of the time, Pallas kernels for 13%

profile of v3, /device:TPU:0, one launch (start us, length us, event | category | flops | bytes accessed | tf_op | source)
XLA Modules:
  0.0 36.7 jit_solution(9289902531072612801)
XLA Ops:
  0.6 2.3 %turn_in.1 = (f32[1920,128]{1,0:T(8,128)S(1)}, f32[640,128]{1,0:T(8,128)S(1)}, f32[1920,128]{1,0:T(8,128)S(1)}, f32[640,128]{1,0:T(8,128)S(1)}, bf16[256,256]{1,...) custom-call(s32[4]{0:T(128)} %length_ref.5, ...), custom_call_target="tpu_custom_call" | custom-call | flops 1048576 | bytes 4194304 | tf_op jit(solution)/shard_map/turn_in/pallas_call | solution.py:359
  2.9 4.1 %collective-permute-start.1 = (f32[192,128]{1,0:T(8,128)S(1)}, f32[192,128]{1,0:T(8,128)S(1)}, u32[]{:S(2)}, u32[]{:S(2)}) collective-permute-start(f32[192,128]{1,0:T(8,128)S(1)} %get-tuple-element.28), channel_id=1, source_target_pairs={{0,16},{2,18},{4,20},{6,22},{8,24},{10,26},{12,28},{14,30},{16,0},... | collective-permute-start | bytes 294920 | tf_op jit(solution)/shard_map/ppermute | solution.py:340
  7.1 1.6 %collective-permute-start = (f32[128,128]{1,0:T(8,128)S(1)}, f32[128,128]{1,0:T(8,128)S(1)}, u32[]{:S(2)}, u32[]{:S(2)}) collective-permute-start(f32[128,128]{1,0:T(8,128)S(1)} %get-tuple-element.25.refs_0_), channel_id=1, source_target_pairs={{0,8},{2,10},{4,12},{6,14},{8,16},{10,18},{12,20},{14,22},{16,24},... | collective-permute-start | bytes 196616 | tf_op jit(solution)/shard_map/ppermute | solution.py:340
  8.7 2.2 %collective-permute-start.2 = (f32[128,128]{1,0:T(8,128)S(1)}, f32[128,128]{1,0:T(8,128)S(1)}, u32[]{:S(2)}, u32[]{:S(2)}) collective-permute-start(f32[128,128]{1,0:T(8,128)S(1)} %get-tuple-element.25.refs_0_), channel_id=1, source_target_pairs={{0,24},{2,26},{4,28},{6,30},{8,0},{10,2},{12,4},{14,6},{16,8},{18,... | collective-permute-start | bytes 196616 | tf_op jit(solution)/shard_map/ppermute | solution.py:340
  10.9 1.5 %collective-permute-start.3 = (f32[64,128]{1,0:T(8,128)S(1)}, f32[64,128]{1,0:T(8,128)S(1)}, u32[]{:S(2)}, u32[]{:S(2)}) collective-permute-start(f32[64,128]{1,0:T(8,128)S(1)} %get-tuple-element.33), channel_id=1, source_target_pairs={{0,1},{1,0},{2,3},{3,2},{4,5},{5,4},{6,7},{7,6},{8,9},{9,8},{10,11... | collective-permute-start | bytes 98312 | tf_op jit(solution)/shard_map/ppermute | solution.py:340
  12.4 0.8 %collective-permute-done.refs_3_ = f32[128,128]{1,0:T(8,128)S(1)} collective-permute-done((f32[128,128]{1,0:T(8,128)S(1)}, f32[128,128]{1,0:T(8,128)S(1)}, u32[]{:S(2)}, u32[]{:S(2)}) %collective-permute-start) | collective-permute-done | bytes 65568 | tf_op jit(solution)/shard_map/ppermute | solution.py:340
  13.2 1.0 %collective-permute-done.2.refs_5_ = f32[128,128]{1,0:T(8,128)S(1)} collective-permute-done((f32[128,128]{1,0:T(8,128)S(1)}, f32[128,128]{1,0:T(8,128)S(1)}, u32[]{:S(2)}, u32[]{:S(2)}) %collective-permute-start.2) | collective-permute-done | bytes 65568 | tf_op jit(solution)/shard_map/ppermute | solution.py:340
  14.3 0.0 collective-permute-done.1.refs_4_.pole
  14.3 0.1 collective-permute-start.4
  14.4 4.4 %collective-permute-start.5 = (f32[192,128]{1,0:T(8,128)S(1)}, f32[192,128]{1,0:T(8,128)S(1)}, u32[]{:S(2)}, u32[]{:S(2)}) collective-permute-start(f32[192,128]{1,0:T(8,128)S(1)} %get-tuple-element.40), channel_id=1, source_target_pairs={{0,30},{2,0},{4,2},{6,4},{8,6},{10,8},{12,10},{14,12},{16,14},{18,... | collective-permute-start | bytes 294920 | tf_op jit(solution)/shard_map/ppermute | solution.py:340
  18.8 0.0 collective-permute-start.6
  18.8 0.0 collective-permute-done.3.lat_a.lat_b
  18.8 1.9 %merid.1.mt = f32[1920,128]{1,0:T(8,128)S(1)} custom-call(f32[1920,128]{1,0:T(8,128)S(1)} %get-tuple-element.30.mt, f32[640,128]{1,0:T(8,128)S(1)} %get-tuple-element.31.mct, bf16[256,256]{1,0:T(8,128)(2,1)S(1)} %get-tuple-element.32.w_ref, f32[192,128]{1,0:T(8,128)S(1)} %collective-permute-done.1.refs_4_.pole, ...), custom_call_target="tpu_custom_call" | custom-call | flops 4294967296 | bytes 4194304 | tf_op jit(solution)/shard_map/merid/pallas_call | solution.py:418
  20.7 0.0 copy-start
  20.7 5.0 %collective-permute-done.6.refs_0_ = f32[128,128]{1,0:T(8,128)S(1)} collective-permute-done((f32[128,128]{1,0:T(8,128)S(1)}, f32[128,128]{1,0:T(8,128)S(1)}, u32[]{:S(2)}, u32[]{:S(2)}) %collective-permute-start.6) | collective-permute-done | bytes 65568 | tf_op jit(solution)/shard_map/ppermute | solution.py:340
  25.8 0.0 collective-permute-done.4.behind
  25.8 0.0 collective-permute-done.5.ahead
  25.8 0.0 copy-done
  25.8 3.0 %zonal.1 = (f32[1920,128]{1,0:T(8,128)S(1)}, f32[4,128]{1,0:T(4,128)S(1)}, f32[16,128]{1,0:T(8,128)S(1)}, f32[4,128]{1,0:T(4,128)S(1)}) custom-call(s32[4]{0:T(128)} %length_ref.5, s32[4,128]{1,0:T(4,128)S(1)} %copy-done, f32[1920,128]{1,0:T(8,128)S(1)} %get-tuple-element.36.zt, f32[640,128]{1,0:T(8,128)S(1)} %get-tuple-element.37.zct, ...), custom_call_target="tpu_custom_call" | custom-call | flops 4294967296 | bytes 4194304 | tf_op jit(solution)/shard_map/zonal/pallas_call | solution.py:423
  28.8 0.1 collective-permute-start.7
  28.9 4.4 %collective-permute-start.8 = (f32[4,128]{1,0:T(4,128)S(1)}, f32[4,128]{1,0:T(4,128)S(1)}, u32[]{:S(2)}, u32[]{:S(2)}) collective-permute-start(f32[4,128]{1,0:T(4,128)S(1)} %get-tuple-element.46), channel_id=1, source_target_pairs={{0,30},{2,0},{4,2},{6,4},{8,6},{10,8},{12,10},{14,12},{16,14},{18,... | collective-permute-start | bytes 6152 | tf_op jit(solution)/shard_map/ppermute | solution.py:340
  33.3 2.8 %turn_out.1 = (f32[1536,128]{1,0:T(8,128)}, f32[1536,128]{1,0:T(8,128)}) custom-call(s32[4]{0:T(128)} %length_ref.5, f32[1536,128]{1,0:T(8,128)} %bitcast.10, f32[1920,128]{1,0:T(8,128)S(1)} %merid.1.mt, f32[1920,128]{1,0:T(8,128)S(1)} %get-tuple-element.41.zt), custom_call_target="tpu_custom_call" | custom-call | flops 4294967296 | bytes 4194304 | tf_op jit(solution)/shard_map/turn_out/pallas_call | solution.py:439
  36.1 0.0 collective-permute-done.7.from_left
  36.1 0.0 collective-permute-done.8.from_right
  36.1 0.6 %finish.1 = f32[16,128]{1,0:T(8,128)} custom-call(f32[16,128]{1,0:T(8,128)S(1)} %get-tuple-element.44.mid, f32[4,128]{1,0:T(4,128)S(1)} %collective-permute-done.7.from_left, f32[4,128]{1,0:T(4,128)S(1)} %collective-permute-done.8.from_right), custom_call_target="tpu_custom_call" | custom-call | flops 1048576 | bytes 4194304 | tf_op jit(solution)/shard_map/finish/pallas_call | solution.py:449
  (1 shorter events, 0.0 us)
Async XLA Ops:
  2.9 11.3 %collective-permute-start.1 = (f32[192,128]{1,0:T(8,128)S(1)}, f32[192,128]{1,0:T(8,128)S(1)}, u32[]{:S(2)}, u32[]{:S(2)}) collective-permute-start(f32[192,128]{1,0:T(8,128)S(1)} %get-tuple-element.28), channel_id=1, source_target_pairs={{0,16},{2,18},{4,20},{6,22},{8,24},{10,26},{12,28},{14,30},{16,0},... | collective-permute-start | bytes 294920 | tf_op jit(solution)/shard_map/ppermute | solution.py:340
  7.1 6.2 %collective-permute-start = (f32[128,128]{1,0:T(8,128)S(1)}, f32[128,128]{1,0:T(8,128)S(1)}, u32[]{:S(2)}, u32[]{:S(2)}) collective-permute-start(f32[128,128]{1,0:T(8,128)S(1)} %get-tuple-element.25.refs_0_), channel_id=1, source_target_pairs={{0,8},{2,10},{4,12},{6,14},{8,16},{10,18},{12,20},{14,22},{16,24},... | collective-permute-start | bytes 196616 | tf_op jit(solution)/shard_map/ppermute | solution.py:340
  8.7 5.6 %collective-permute-start.2 = (f32[128,128]{1,0:T(8,128)S(1)}, f32[128,128]{1,0:T(8,128)S(1)}, u32[]{:S(2)}, u32[]{:S(2)}) collective-permute-start(f32[128,128]{1,0:T(8,128)S(1)} %get-tuple-element.25.refs_0_), channel_id=1, source_target_pairs={{0,24},{2,26},{4,28},{6,30},{8,0},{10,2},{12,4},{14,6},{16,8},{18,... | collective-permute-start | bytes 196616 | tf_op jit(solution)/shard_map/ppermute | solution.py:340
  10.9 7.9 %collective-permute-start.3 = (f32[64,128]{1,0:T(8,128)S(1)}, f32[64,128]{1,0:T(8,128)S(1)}, u32[]{:S(2)}, u32[]{:S(2)}) collective-permute-start(f32[64,128]{1,0:T(8,128)S(1)} %get-tuple-element.33), channel_id=1, source_target_pairs={{0,1},{1,0},{2,3},{3,2},{4,5},{5,4},{6,7},{7,6},{8,9},{9,8},{10,11... | collective-permute-start | bytes 98312 | tf_op jit(solution)/shard_map/ppermute | solution.py:340
  14.3 11.5 %collective-permute-start.4 = (f32[192,128]{1,0:T(8,128)S(1)}, f32[192,128]{1,0:T(8,128)S(1)}, u32[]{:S(2)}, u32[]{:S(2)}) collective-permute-start(f32[192,128]{1,0:T(8,128)S(1)} %get-tuple-element.39), channel_id=1, source_target_pairs={{0,2},{2,4},{4,6},{6,8},{8,10},{10,12},{12,14},{14,16},{16,18},{18... | collective-permute-start | bytes 294920 | tf_op jit(solution)/shard_map/ppermute | solution.py:340
  14.4 11.4 %collective-permute-start.5 = (f32[192,128]{1,0:T(8,128)S(1)}, f32[192,128]{1,0:T(8,128)S(1)}, u32[]{:S(2)}, u32[]{:S(2)}) collective-permute-start(f32[192,128]{1,0:T(8,128)S(1)} %get-tuple-element.40), channel_id=1, source_target_pairs={{0,30},{2,0},{4,2},{6,4},{8,6},{10,8},{12,10},{14,12},{16,14},{18,... | collective-permute-start | bytes 294920 | tf_op jit(solution)/shard_map/ppermute | solution.py:340
  18.8 7.0 %collective-permute-start.6 = (f32[128,128]{1,0:T(8,128)S(1)}, f32[128,128]{1,0:T(8,128)S(1)}, u32[]{:S(2)}, u32[]{:S(2)}) collective-permute-start(f32[128,128]{1,0:T(8,128)S(1)} %get-tuple-element.38.own), channel_id=1, source_target_pairs={{0,4},{2,6},{4,8},{6,10},{8,12},{10,14},{12,16},{14,18},{16,20},{1... | collective-permute-start | bytes 196616 | tf_op jit(solution)/shard_map/ppermute | solution.py:340
  20.7 5.1 %copy-start = (s32[4,128]{1,0:T(4,128)S(1)}, s32[4,128]{1,0:T(4,128)}, u32[]{:S(2)}) copy-start(s32[4,128]{1,0:T(4,128)} %owner_ref.1) | copy-start | bytes 6148
  28.8 7.3 %collective-permute-start.7 = (f32[4,128]{1,0:T(4,128)S(1)}, f32[4,128]{1,0:T(4,128)S(1)}, u32[]{:S(2)}, u32[]{:S(2)}) collective-permute-start(f32[4,128]{1,0:T(4,128)S(1)} %get-tuple-element.45), channel_id=1, source_target_pairs={{0,2},{2,4},{4,6},{6,8},{8,10},{10,12},{12,14},{14,16},{16,18},{18... | collective-permute-start | bytes 6152 | tf_op jit(solution)/shard_map/ppermute | solution.py:340
  28.9 7.2 %collective-permute-start.8 = (f32[4,128]{1,0:T(4,128)S(1)}, f32[4,128]{1,0:T(4,128)S(1)}, u32[]{:S(2)}, u32[]{:S(2)}) collective-permute-start(f32[4,128]{1,0:T(4,128)S(1)} %get-tuple-element.46), channel_id=1, source_target_pairs={{0,30},{2,0},{4,2},{6,4},{8,6},{10,8},{12,10},{14,12},{16,14},{18,... | collective-permute-start | bytes 6152 | tf_op jit(solution)/shard_map/ppermute | solution.py:340

commit v4 on v3

--- a/solution.py
+++ b/solution.py
@@ -283,11 +283,8 @@
             mid_ref[g * sz.rows + r : g * sz.rows + r + 1, :] = sums[g + 1 : g + 2]
 
 
-def turn_out(sz, length_ref, z_ref, mt, zt, m_out, z_out, m_own, z_own, z_in, length, sems):
-    reads = [
-        pltpu.make_async_copy(length_ref, length, sems.at[0]),
-        pltpu.make_async_copy(z_ref, z_in, sems.at[1]),
-    ]
+def turn_out(sz, length_ref, z_ref, mt, zt, m_out, z_out, m_own, z_own, length, sems):
+    reads = [pltpu.make_async_copy(length_ref, length, sems.at[0])]
     for copy in reads:
         copy.start()
     writes = []
@@ -307,9 +304,9 @@
                 value = jnp.concatenate(halves, axis=0).T
                 at = pl.ds(w * sz.rows + r, sz.lanes, stride=sz.wr)
                 if zonal:
-                    value = jnp.where(cell < length[r], value, z_in[at, :])
+                    value = jnp.where(cell < length[r], value, z_ref[at, :])
                 dst[at, :] = value
-        writes.append(pltpu.make_async_copy(dst, out, sems.at[2 + zonal]))
+        writes.append(pltpu.make_async_copy(dst, out, sems.at[1 + zonal]))
         writes[-1].start()
     for copy in writes:
         copy.wait()
@@ -438,14 +435,13 @@
     from_left = shifted(above, "lon", 1)
     m_next, z_next = call(
         functools.partial(turn_out, sz),
-        (f32(*m.shape), f32(*z.shape)), [pltpu.HBM] * 2 + [pltpu.VMEM] * 2,
+        (f32(*m.shape), f32(*z.shape)), [pltpu.HBM] + [pltpu.VMEM] * 3,
         (
             pltpu.VMEM(m.shape, jnp.float32), pltpu.VMEM(z.shape, jnp.float32),
-            pltpu.VMEM(z.shape, jnp.float32), pltpu.SMEM((sz.rows,), jnp.int32),
-            pltpu.SemaphoreType.DMA((4,)),
+            pltpu.SMEM((sz.rows,), jnp.int32), pltpu.SemaphoreType.DMA((3,)),
         ),
         "turn_out", 1 << 32, pltpu.HBM,
-    )(zonal_length, z, mt_next, zt_next)
+    )(zonal_length, flat(zonal_state), mt_next, zt_next)
     (coupling,) = call(
         functools.partial(finish, sz), (f32(*mid.shape),), [pltpu.VMEM] * 3, (), "finish",
     )(mid, from_left, from_right)

time: 36.9 us -> 36.4 us (0.986)
    pallas_call x1, Pallas kernels: 2.78 us -> 1.88 us  [shards(): call(functools.partial(turn_out, sz), (f32(*m.shape), f32(*z.shape)), [pl...]
    pallas_call x1, Pallas kernels: 3.03 us -> 3.42 us  [shards(): call(functools.partial(zonal_kernel, sz, len(others)), (f32(state_rows, l...]
  transfers between devices with their start and end apart: 9 -> 9, of which waited for: 3 -> 3; matrix products, arithmetic and copies ran while one was open for 0% -> 0% of each run, Pallas kernels for 13% -> 11%
where the time goes in v4:
time: 36.4 us; the launch traced here: 36.2 us
  starting transfers between devices  18.5 us (51%)
  Pallas kernels  10.4 us (29%)
  waiting for transfers between devices  6.67 us (18%)
  between operations  0.73 us (2%)
    ppermute x9, starting transfers between devices, shifted(): lax.ppermute(value, axis, [(i, (i + steps) % count) for i in range(count)])  18.5 us
    ppermute x9, waiting for transfers between devices, shifted(): lax.ppermute(value, axis, [(i, (i + steps) % count) for i in range(count)])  6.67 us
    pallas_call x1, Pallas kernels, shards(): call(functools.partial(zonal_kernel, sz, len(others)), (f32(state_rows, l...  3.42 us
    pallas_call x1, Pallas kernels, shards(): call(functools.partial(turn_in, sz, lat_two, lat_count), (f32(state_rows,...  2.31 us
    pallas_call x1, Pallas kernels, shards(): call(functools.partial(merid_kernel, sz, lat_two, lat_count), (f32(state_...  2.14 us
    pallas_call x1, Pallas kernels, shards(): call(functools.partial(turn_out, sz), (f32(*m.shape), f32(*z.shape)), [pl...  1.88 us
  transfers between devices with their start and end apart: 9, of which 3 were waited for; matrix products, arithmetic and copies ran while one was open for 0% of the time, Pallas kernels for 11%

profile of v4, /device:TPU:0, one launch (start us, length us, event | category | flops | bytes accessed | tf_op | source)
XLA Modules:
  0.0 36.2 jit_solution(7007798488885879183)
XLA Ops:
  0.6 2.3 %turn_in.1 = (f32[1920,128]{1,0:T(8,128)S(1)}, f32[640,128]{1,0:T(8,128)S(1)}, f32[1920,128]{1,0:T(8,128)S(1)}, f32[640,128]{1,0:T(8,128)S(1)}, bf16[256,256]{1,...) custom-call(s32[4]{0:T(128)} %length_ref.5, ...), custom_call_target="tpu_custom_call" | custom-call | flops 1048576 | bytes 4194304 | tf_op jit(solution)/shard_map/turn_in/pallas_call | solution.py:356
  2.9 4.1 %collective-permute-start.1 = (f32[192,128]{1,0:T(8,128)S(1)}, f32[192,128]{1,0:T(8,128)S(1)}, u32[]{:S(2)}, u32[]{:S(2)}) collective-permute-start(f32[192,128]{1,0:T(8,128)S(1)} %get-tuple-element.28), channel_id=1, source_target_pairs={{0,16},{2,18},{4,20},{6,22},{8,24},{10,26},{12,28},{14,30},{16,0},... | collective-permute-start | bytes 294920 | tf_op jit(solution)/shard_map/ppermute | solution.py:337
  7.1 1.6 %collective-permute-start = (f32[128,128]{1,0:T(8,128)S(1)}, f32[128,128]{1,0:T(8,128)S(1)}, u32[]{:S(2)}, u32[]{:S(2)}) collective-permute-start(f32[128,128]{1,0:T(8,128)S(1)} %get-tuple-element.25.refs_0_), channel_id=1, source_target_pairs={{0,8},{2,10},{4,12},{6,14},{8,16},{10,18},{12,20},{14,22},{16,24},... | collective-permute-start | bytes 196616 | tf_op jit(solution)/shard_map/ppermute | solution.py:337
  8.7 2.2 %collective-permute-start.2 = (f32[128,128]{1,0:T(8,128)S(1)}, f32[128,128]{1,0:T(8,128)S(1)}, u32[]{:S(2)}, u32[]{:S(2)}) collective-permute-start(f32[128,128]{1,0:T(8,128)S(1)} %get-tuple-element.25.refs_0_), channel_id=1, source_target_pairs={{0,24},{2,26},{4,28},{6,30},{8,0},{10,2},{12,4},{14,6},{16,8},{18,... | collective-permute-start | bytes 196616 | tf_op jit(solution)/shard_map/ppermute | solution.py:337
  10.9 1.5 %collective-permute-start.3 = (f32[64,128]{1,0:T(8,128)S(1)}, f32[64,128]{1,0:T(8,128)S(1)}, u32[]{:S(2)}, u32[]{:S(2)}) collective-permute-start(f32[64,128]{1,0:T(8,128)S(1)} %get-tuple-element.33), channel_id=1, source_target_pairs={{0,1},{1,0},{2,3},{3,2},{4,5},{5,4},{6,7},{7,6},{8,9},{9,8},{10,11... | collective-permute-start | bytes 98312 | tf_op jit(solution)/shard_map/ppermute | solution.py:337
  12.4 0.8 %collective-permute-done.refs_3_ = f32[128,128]{1,0:T(8,128)S(1)} collective-permute-done((f32[128,128]{1,0:T(8,128)S(1)}, f32[128,128]{1,0:T(8,128)S(1)}, u32[]{:S(2)}, u32[]{:S(2)}) %collective-permute-start) | collective-permute-done | bytes 65568 | tf_op jit(solution)/shard_map/ppermute | solution.py:337
  13.2 1.0 %collective-permute-done.2.refs_5_ = f32[128,128]{1,0:T(8,128)S(1)} collective-permute-done((f32[128,128]{1,0:T(8,128)S(1)}, f32[128,128]{1,0:T(8,128)S(1)}, u32[]{:S(2)}, u32[]{:S(2)}) %collective-permute-start.2) | collective-permute-done | bytes 65568 | tf_op jit(solution)/shard_map/ppermute | solution.py:337
  14.3 0.0 collective-permute-done.1.refs_4_.pole
  14.3 0.1 collective-permute-start.4
  14.4 4.4 %collective-permute-start.5 = (f32[192,128]{1,0:T(8,128)S(1)}, f32[192,128]{1,0:T(8,128)S(1)}, u32[]{:S(2)}, u32[]{:S(2)}) collective-permute-start(f32[192,128]{1,0:T(8,128)S(1)} %get-tuple-element.40), channel_id=1, source_target_pairs={{0,30},{2,0},{4,2},{6,4},{8,6},{10,8},{12,10},{14,12},{16,14},{18,... | collective-permute-start | bytes 294920 | tf_op jit(solution)/shard_map/ppermute | solution.py:337
  18.8 0.0 collective-permute-start.6
  18.8 0.0 collective-permute-done.3.lat_a.lat_b
  18.8 2.1 %merid.1.mt = f32[1920,128]{1,0:T(8,128)S(1)} custom-call(f32[1920,128]{1,0:T(8,128)S(1)} %get-tuple-element.30.mt, f32[640,128]{1,0:T(8,128)S(1)} %get-tuple-element.31.mct, bf16[256,256]{1,0:T(8,128)(2,1)S(1)} %get-tuple-element.32.w_ref, f32[192,128]{1,0:T(8,128)S(1)} %collective-permute-done.1.refs_4_.pole, ...), custom_call_target="tpu_custom_call" | custom-call | flops 4294967296 | bytes 4194304 | tf_op jit(solution)/shard_map/merid/pallas_call | solution.py:415
  21.0 0.0 copy-start.1
  21.0 4.8 %collective-permute-done.6.refs_0_ = f32[128,128]{1,0:T(8,128)S(1)} collective-permute-done((f32[128,128]{1,0:T(8,128)S(1)}, f32[128,128]{1,0:T(8,128)S(1)}, u32[]{:S(2)}, u32[]{:S(2)}) %collective-permute-start.6) | collective-permute-done | bytes 65568 | tf_op jit(solution)/shard_map/ppermute | solution.py:337
  25.8 0.0 collective-permute-done.4.behind
  25.8 0.0 collective-permute-done.5.ahead
  25.8 0.0 copy-done.1
  25.8 0.0 copy-start
  25.8 3.4 %zonal.1 = (f32[1920,128]{1,0:T(8,128)S(1)}, f32[4,128]{1,0:T(4,128)S(1)}, f32[16,128]{1,0:T(8,128)S(1)}, f32[4,128]{1,0:T(4,128)S(1)}) custom-call(s32[4]{0:T(128)} %length_ref.5, s32[4,128]{1,0:T(4,128)S(1)} %copy-done.1, f32[1920,128]{1,0:T(8,128)S(1)} %get-tuple-element.36.zt, f32[640,128]{1,0:T(8,128)S(1)} %get-tuple-element.37.zct, ...), custom_call_target="tpu_custom_call" | custom-call | flops 4294967296 | bytes 4194304 | tf_op jit(solution)/shard_map/zonal/pallas_call | solution.py:420
  29.2 0.1 collective-permute-start.7
  29.3 4.4 %collective-permute-start.8 = (f32[4,128]{1,0:T(4,128)S(1)}, f32[4,128]{1,0:T(4,128)S(1)}, u32[]{:S(2)}, u32[]{:S(2)}) collective-permute-start(f32[4,128]{1,0:T(4,128)S(1)} %get-tuple-element.46), channel_id=1, source_target_pairs={{0,30},{2,0},{4,2},{6,4},{8,6},{10,8},{12,10},{14,12},{16,14},{18,... | collective-permute-start | bytes 6152 | tf_op jit(solution)/shard_map/ppermute | solution.py:337
  33.7 0.0 copy-done
  33.7 1.9 %turn_out.1 = (f32[1536,128]{1,0:T(8,128)}, f32[1536,128]{1,0:T(8,128)}) custom-call(s32[4]{0:T(128)} %length_ref.5, f32[1536,128]{1,0:T(8,128)S(1)} %bitcast.9, f32[1920,128]{1,0:T(8,128)S(1)} %merid.1.mt, f32[1920,128]{1,0:T(8,128)S(1)} %get-tuple-element.41.zt), custom_call_target="tpu_custom_call" | custom-call | flops 4294967296 | bytes 4194304 | tf_op jit(solution)/shard_map/turn_out/pallas_call | solution.py:436
  35.6 0.0 collective-permute-done.7.from_left
  35.6 0.0 collective-permute-done.8.from_right
  35.6 0.6 %finish.1 = f32[16,128]{1,0:T(8,128)} custom-call(f32[16,128]{1,0:T(8,128)S(1)} %get-tuple-element.44.mid, f32[4,128]{1,0:T(4,128)S(1)} %collective-permute-done.7.from_left, f32[4,128]{1,0:T(4,128)S(1)} %collective-permute-done.8.from_right), custom_call_target="tpu_custom_call" | custom-call | flops 1048576 | bytes 4194304 | tf_op jit(solution)/shard_map/finish/pallas_call | solution.py:445
  (1 shorter events, 0.0 us)
Async XLA Ops:
  2.9 11.3 %collective-permute-start.1 = (f32[192,128]{1,0:T(8,128)S(1)}, f32[192,128]{1,0:T(8,128)S(1)}, u32[]{:S(2)}, u32[]{:S(2)}) collective-permute-start(f32[192,128]{1,0:T(8,128)S(1)} %get-tuple-element.28), channel_id=1, source_target_pairs={{0,16},{2,18},{4,20},{6,22},{8,24},{10,26},{12,28},{14,30},{16,0},... | collective-permute-start | bytes 294920 | tf_op jit(solution)/shard_map/ppermute | solution.py:337
  7.1 6.2 %collective-permute-start = (f32[128,128]{1,0:T(8,128)S(1)}, f32[128,128]{1,0:T(8,128)S(1)}, u32[]{:S(2)}, u32[]{:S(2)}) collective-permute-start(f32[128,128]{1,0:T(8,128)S(1)} %get-tuple-element.25.refs_0_), channel_id=1, source_target_pairs={{0,8},{2,10},{4,12},{6,14},{8,16},{10,18},{12,20},{14,22},{16,24},... | collective-permute-start | bytes 196616 | tf_op jit(solution)/shard_map/ppermute | solution.py:337
  8.7 5.6 %collective-permute-start.2 = (f32[128,128]{1,0:T(8,128)S(1)}, f32[128,128]{1,0:T(8,128)S(1)}, u32[]{:S(2)}, u32[]{:S(2)}) collective-permute-start(f32[128,128]{1,0:T(8,128)S(1)} %get-tuple-element.25.refs_0_), channel_id=1, source_target_pairs={{0,24},{2,26},{4,28},{6,30},{8,0},{10,2},{12,4},{14,6},{16,8},{18,... | collective-permute-start | bytes 196616 | tf_op jit(solution)/shard_map/ppermute | solution.py:337
  10.9 7.9 %collective-permute-start.3 = (f32[64,128]{1,0:T(8,128)S(1)}, f32[64,128]{1,0:T(8,128)S(1)}, u32[]{:S(2)}, u32[]{:S(2)}) collective-permute-start(f32[64,128]{1,0:T(8,128)S(1)} %get-tuple-element.33), channel_id=1, source_target_pairs={{0,1},{1,0},{2,3},{3,2},{4,5},{5,4},{6,7},{7,6},{8,9},{9,8},{10,11... | collective-permute-start | bytes 98312 | tf_op jit(solution)/shard_map/ppermute | solution.py:337
  14.3 11.5 %collective-permute-start.4 = (f32[192,128]{1,0:T(8,128)S(1)}, f32[192,128]{1,0:T(8,128)S(1)}, u32[]{:S(2)}, u32[]{:S(2)}) collective-permute-start(f32[192,128]{1,0:T(8,128)S(1)} %get-tuple-element.39), channel_id=1, source_target_pairs={{0,2},{2,4},{4,6},{6,8},{8,10},{10,12},{12,14},{14,16},{16,18},{18... | collective-permute-start | bytes 294920 | tf_op jit(solution)/shard_map/ppermute | solution.py:337
  14.4 11.4 %collective-permute-start.5 = (f32[192,128]{1,0:T(8,128)S(1)}, f32[192,128]{1,0:T(8,128)S(1)}, u32[]{:S(2)}, u32[]{:S(2)}) collective-permute-start(f32[192,128]{1,0:T(8,128)S(1)} %get-tuple-element.40), channel_id=1, source_target_pairs={{0,30},{2,0},{4,2},{6,4},{8,6},{10,8},{12,10},{14,12},{16,14},{18,... | collective-permute-start | bytes 294920 | tf_op jit(solution)/shard_map/ppermute | solution.py:337
  18.8 7.0 %collective-permute-start.6 = (f32[128,128]{1,0:T(8,128)S(1)}, f32[128,128]{1,0:T(8,128)S(1)}, u32[]{:S(2)}, u32[]{:S(2)}) collective-permute-start(f32[128,128]{1,0:T(8,128)S(1)} %get-tuple-element.38.own), channel_id=1, source_target_pairs={{0,4},{2,6},{4,8},{6,10},{8,12},{10,14},{12,16},{14,18},{16,20},{1... | collective-permute-start | bytes 196616 | tf_op jit(solution)/shard_map/ppermute | solution.py:337
  21.0 4.8 %copy-start.1 = (s32[4,128]{1,0:T(4,128)S(1)}, s32[4,128]{1,0:T(4,128)}, u32[]{:S(2)}) copy-start(s32[4,128]{1,0:T(4,128)} %owner_ref.1) | copy-start | bytes 6148
  25.8 7.9 %copy-start = (f32[4,32,3,4,128]{4,3,2,1,0:T(4,128)S(1)}, f32[4,32,3,4,128]{4,3,2,1,0:T(4,128)}, u32[]{:S(2)}) copy-start(f32[4,32,3,4,128]{4,3,2,1,0:T(4,128)} %param.7) | copy-start | bytes 2359300
  29.2 6.4 %collective-permute-start.7 = (f32[4,128]{1,0:T(4,128)S(1)}, f32[4,128]{1,0:T(4,128)S(1)}, u32[]{:S(2)}, u32[]{:S(2)}) collective-permute-start(f32[4,128]{1,0:T(4,128)S(1)} %get-tuple-element.45), channel_id=1, source_target_pairs={{0,2},{2,4},{4,6},{6,8},{8,10},{10,12},{12,14},{14,16},{16,18},{18... | collective-permute-start | bytes 6152 | tf_op jit(solution)/shard_map/ppermute | solution.py:337
  29.3 6.3 %collective-permute-start.8 = (f32[4,128]{1,0:T(4,128)S(1)}, f32[4,128]{1,0:T(4,128)S(1)}, u32[]{:S(2)}, u32[]{:S(2)}) collective-permute-start(f32[4,128]{1,0:T(4,128)S(1)} %get-tuple-element.46), channel_id=1, source_target_pairs={{0,30},{2,0},{4,2},{6,4},{8,6},{10,8},{12,10},{14,12},{16,14},{18,... | collective-permute-start | bytes 6152 | tf_op jit(solution)/shard_map/ppermute | solution.py:337
